TPU v7x, 32 devices: a whole 2x2x4 slice. The times are simulated.
32 devices in a mesh: seq: 8 (over z, x), head: 4 (over y, core).
Axes of the slice: x: 2, y: 2, z: 4, core: 2. Of those that a mesh axis runs over, the one named last changes fastest.
Arguments:
- inputs: bfloat16 [24, 1024, 512], P('seq', 'head'), may hold values from -6 to 6
- cotangent: bfloat16 [24, 1024, 512], P('seq', 'head'), may hold values from -6 to 6
- span_offset: int32 [24, 64], P('seq', 'head'), may hold values from 0 to 8
- span_len: int32 [24, 64], P('seq', 'head'), may hold values from 1 to 8
- owner_slot: int32 [256], replicated, may hold values from 0 to 255, as said below
- master: float32 [256, 128, 128], P(('seq', 'head')), as said below
- moment_one: float32 [256, 128, 128], P(('seq', 'head')), as said below
- moment_two: float32 [256, 128, 128], P(('seq', 'head')), may hold values from 294.912 to 29491.2, as said below
- basis_left: float32 [256, 128, 128], P(('seq', 'head')), may hold values from -1 to 1, as said below
- basis_right: float32 [256, 128, 128], P(('seq', 'head')), may hold values from -1 to 1, as said below
- average: float32 [256, 128, 128], P(('seq', 'head')), may hold values from -0.25 to 0.25
- vec_master: float32 [6144], P(('seq', 'head')), as said below
- vec_moment_one: float32 [6144], P(('seq', 'head')), may hold values from -343.46005 to 343.46005
- vec_moment_two: float32 [6144], P(('seq', 'head')), may hold values from 7372.8 to 29491.2
Outputs:
- layer_out: bfloat16 [24, 1024, 512], P('seq', 'head')
- input_grad: float32 [24, 1024, 512], P('seq', 'head')
- slot_grad: float32 [256, 128, 128], P(('seq', 'head'))
- vec_grad: float32 [6144], P(('seq', 'head'))
- new_moment_one: float32 [256, 128, 128], P(('seq', 'head'))
- new_moment_two: float32 [256, 128, 128], P(('seq', 'head'))
- new_master: float32 [256, 128, 128], P(('seq', 'head'))
- new_master_bf16: bfloat16 [256, 128, 128], P(('seq', 'head'))
- new_average: float32 [256, 128, 128], P(('seq', 'head'))
- new_vec_moment_one: float32 [6144], P(('seq', 'head'))
- new_vec_moment_two: float32 [6144], P(('seq', 'head'))
- new_vec: float32 [6144], P(('seq', 'head'))
Inputs may be any that keep to these rules, and one draw needn't show every extreme that they name: `owner_slot`: A permutation of the slots; values of 192 or more mark empty slots. `master`: Real-valued blocks. `moment_one`: Real-valued, of both signs. `moment_two`: Positive. `basis_left`: each block is orthogonal. `basis_right`: each block is orthogonal. `vec_master`: the gains g_1 and g_2 are positive.
All inputs are finite; a program needn't handle non-finite values.
Results may differ from a plain program's by a relative error of at most 0.013.
The roundings to bfloat16 on the way count: a program that leaves them out, or rounds other values in their place, can miss the bound.
Values may be sent and summed in bfloat16 or wider, within the bound.
A program may use at most 128 MiB of HBM per device.

v0:
```python
import math

import jax
import jax.numpy as jnp
from jax import lax
from jax.sharding import PartitionSpec as P

D = 512
FF = 2048
WIN = 16
BLK = 128
STEP = 5
HD = 64
NBLK = 192


NORM_EPS = 1e-06
ADAM_EPS = 1e-08
RATE = 0.05
VEC_RATE = 0.2
DECAY = 0.01
KEEP = 0.9
HIGH = lax.Precision.HIGHEST


def as_sent(array):

    def short(part):
        return part.astype(jnp.bfloat16) if part.dtype == jnp.float32 else part

    return jax.tree.map(short, array)


def split_matrices(blocks):
    rows_d = D // BLK
    cols_f = FF // BLK
    square = rows_d * rows_d

    def build(pieces, row_count, col_count):
        return (
            pieces.reshape(row_count, col_count, BLK, BLK)
            .transpose(0, 2, 1, 3)
            .reshape(row_count * BLK, col_count * BLK)
        )

    matrices = [
        build(blocks[number * square : (number + 1) * square], rows_d, rows_d)
        for number in range(4)
    ]
    offset = 4 * square
    matrices.append(build(blocks[offset : offset + rows_d * cols_f], rows_d, cols_f))
    matrices.append(
        build(blocks[offset + rows_d * cols_f : offset + 2 * rows_d * cols_f], cols_f, rows_d)
    )
    return matrices


def join_matrices(matrices):
    pieces = []
    for matrix in matrices:
        row_count = matrix.shape[0] // BLK
        col_count = matrix.shape[1] // BLK
        pieces.append(
            matrix.reshape(row_count, BLK, col_count, BLK)
            .transpose(0, 2, 1, 3)
            .reshape(row_count * col_count, BLK, BLK)
        )
    return jnp.concatenate(pieces, 0)


def split_vector(vector):
    widths = [D, D, D, D, D, FF, D, D, D]
    pieces = []
    offset = 0
    for extent in widths:
        pieces.append(vector[offset : offset + extent])
        offset = offset + extent
    return pieces


def layer_norm(values, gain, shift):
    center = values - jnp.mean(values, axis=-1, keepdims=True)
    spread = jnp.mean(center * center, axis=-1, keepdims=True)
    return center * lax.rsqrt(spread + NORM_EPS) * gain + shift


def gelu_value(values):
    return 0.5 * values * (1.0 + lax.erf(values * 0.7071067811865476))


def gelu_slope(values):
    return (
        0.5 * (1.0 + lax.erf(values * 0.7071067811865476))
        + values * jnp.exp(-0.5 * values * values) * 0.3989422804014327
    )


def span_mask(span_offset, span_len):
    offsets = jnp.repeat(span_offset, WIN, axis=1)
    extents = jnp.repeat(span_len, WIN, axis=1)
    within = (jnp.arange(offsets.shape[1], dtype=jnp.int32) % WIN)[None, :]
    return ((within >= offsets) & (within < offsets + extents)).astype(jnp.float32)


def attend_forward(query, keys_in, values_in, scale):
    length_full = query.shape[0]
    block = min(512, length_full)
    outputs = []
    totals = []
    for begin_row in range(0, length_full, block):
        scores = (
            jnp.einsum(
                "qhd,khd->hqk",
                query[begin_row : begin_row + block],
                keys_in,
                preferred_element_type=jnp.float32,
            )
            * scale
        )
        highest = jnp.max(scores, axis=-1, keepdims=True)
        weights_exp = jnp.exp(scores - highest)
        summed = jnp.sum(weights_exp, axis=-1, keepdims=True)
        probs = (weights_exp / summed).astype(jnp.bfloat16)
        outputs.append(
            jnp.einsum("hqk,khd->qhd", probs, values_in, preferred_element_type=jnp.float32)
        )
        totals.append(highest + jnp.log(summed))
    return (jnp.concatenate(outputs, 0).astype(jnp.bfloat16), jnp.concatenate(totals, 1))


def attend_backward(query, keys_in, values_in, grad_ctx, log_total, scale):
    length_full = query.shape[0]
    block = min(512, length_full)
    grad_keys = jnp.zeros(keys_in.shape, jnp.float32)
    grad_values = jnp.zeros(values_in.shape, jnp.float32)
    grad_queries = []
    for begin_row in range(0, length_full, block):
        rows_query = query[begin_row : begin_row + block]
        rows_grad = grad_ctx[begin_row : begin_row + block]
        scores = (
            jnp.einsum("qhd,khd->hqk", rows_query, keys_in, preferred_element_type=jnp.float32)
            * scale
        )
        probs = jnp.exp(scores - log_total[:, begin_row : begin_row + block])
        grad_probs = jnp.einsum(
            "qhd,khd->hqk", rows_grad, values_in, preferred_element_type=jnp.float32
        )
        inner = jnp.sum(probs * grad_probs, axis=-1, keepdims=True)
        grad_scores = (probs * (grad_probs - inner)).astype(jnp.bfloat16)
        grad_queries.append(
            jnp.einsum("hqk,khd->qhd", grad_scores, keys_in, preferred_element_type=jnp.float32)
            * scale
        )
        grad_keys = (
            grad_keys
            + jnp.einsum(
                "hqk,qhd->khd", grad_scores, rows_query, preferred_element_type=jnp.float32
            )
            * scale
        )
        grad_values = grad_values + jnp.einsum(
            "hqk,qhd->khd",
            probs.astype(jnp.bfloat16),
            rows_grad,
            preferred_element_type=jnp.float32,
        )
    return (
        jnp.concatenate(grad_queries, 0).astype(jnp.bfloat16),
        grad_keys.astype(jnp.bfloat16),
        grad_values.astype(jnp.bfloat16),
    )


def rotate_adam(grads, master, moment_one, moment_two, basis_left, basis_right):
    rotated = jnp.einsum("sji,sjk->sik", basis_left, grads, precision=HIGH)
    rotated = jnp.einsum("sik,skl->sil", rotated, basis_right, precision=HIGH)
    first = 0.5 * moment_one + 0.5 * rotated
    second = 0.5 * moment_two + 0.5 * rotated * rotated
    correct = 1.0 - 0.5**STEP
    normed = first / correct / (jnp.sqrt(second / correct) + ADAM_EPS)
    turned = jnp.einsum("sij,sjk->sik", basis_left, normed, precision=HIGH)
    turned = jnp.einsum("sik,slk->sil", turned, basis_right, precision=HIGH)
    updated = master - RATE * (turned + DECAY * master)
    return (first, second, updated)


def weight_grad(left, right):
    return jnp.einsum("ti,to->io", left, right, preferred_element_type=jnp.float32)


def back_product(grads, weight):
    return jnp.einsum("to,io->ti", grads, weight, preferred_element_type=jnp.float32)


def body(
    inputs,
    cotangent,
    span_offset,
    span_len,
    owner_slot,
    master,
    moment_one,
    moment_two,
    basis_left,
    basis_right,
    average,
    vec_master,
    vec_moment_one,
    vec_moment_two,
):
    all_slots, all_vector = (
        lax.all_gather(master, ("seq", "head"), axis=0, tiled=True),
        lax.all_gather(vec_master, ("seq", "head"), axis=0, tiled=True),
    )
    slot_total = all_slots.shape[0]
    inverse = (
        jnp.zeros((slot_total,), jnp.int32)
        .at[owner_slot]
        .set(jnp.arange(slot_total, dtype=jnp.int32))
    )
    matrices = split_matrices(all_slots[inverse[:NBLK]])
    w_query, w_key, w_value, w_out, w_up, w_down = [
        matrix.astype(jnp.bfloat16) for matrix in matrices
    ]
    b_query, b_value, b_out, gain_one, shift_one, b_up, b_down, gain_two, shift_two = split_vector(
        all_vector
    )
    seq_local, tok_local, width = inputs.shape
    token_rows = inputs.reshape(seq_local * tok_local, width)
    local_shape = (seq_local, tok_local, width)
    queries = (
        (jnp.dot(token_rows, w_query, preferred_element_type=jnp.float32) + b_query)
        .astype(jnp.bfloat16)
        .reshape(local_shape)
    )
    keys_all = (
        jnp.dot(token_rows, w_key, preferred_element_type=jnp.float32)
        .astype(jnp.bfloat16)
        .reshape(local_shape)
    )
    values_all = (
        (jnp.dot(token_rows, w_value, preferred_element_type=jnp.float32) + b_value)
        .astype(jnp.bfloat16)
        .reshape(local_shape)
    )
    q_heads, k_heads, v_heads = (
        lax.all_to_all(queries, "head", split_axis=2, concat_axis=1, tiled=True),
        lax.all_to_all(keys_all, "head", split_axis=2, concat_axis=1, tiled=True),
        lax.all_to_all(values_all, "head", split_axis=2, concat_axis=1, tiled=True),
    )
    length_full = q_heads.shape[1]
    head_local = q_heads.shape[2] // HD
    scale = 1.0 / math.sqrt(HD)
    split_shape = (seq_local, length_full, head_local, HD)
    q_split = q_heads.reshape(split_shape)
    k_split = k_heads.reshape(split_shape)
    v_split = v_heads.reshape(split_shape)

    def forward_item(items):
        return attend_forward(items[0], items[1], items[2], scale)

    context, log_total = lax.map(forward_item, (q_split, k_split, v_split))
    context = context.reshape(seq_local, length_full, head_local * HD)
    context_local = lax.all_to_all(
        as_sent(context), "head", split_axis=1, concat_axis=2, tiled=True
    ).astype(context.dtype)
    context_rows = context_local.reshape(seq_local * tok_local, width)
    branch = jnp.dot(context_rows, w_out, preferred_element_type=jnp.float32) + b_out
    z_one = token_rows.astype(jnp.float32) + branch
    first = layer_norm(z_one, gain_one, shift_one)
    first_low = first.astype(jnp.bfloat16)
    hidden_in = jnp.dot(first_low, w_up, preferred_element_type=jnp.float32) + b_up
    hidden_act = gelu_value(hidden_in).astype(jnp.bfloat16)
    ffn_out = jnp.dot(hidden_act, w_down, preferred_element_type=jnp.float32) + b_down
    z_two = first + ffn_out
    result, pull_two = jax.vjp(layer_norm, z_two, gain_two, shift_two)
    layer_out = result.astype(jnp.bfloat16).reshape(local_shape)
    mask = span_mask(span_offset, span_len)
    grad_out = (cotangent.astype(jnp.float32) * mask[:, :, None]).reshape(
        seq_local * tok_local, width
    )
    d_ztwo, d_gain_two, d_shift_two = pull_two(grad_out)
    d_ffn = d_ztwo.astype(jnp.bfloat16)
    grad_down = weight_grad(hidden_act, d_ffn)
    grad_bdown = jnp.sum(d_ffn.astype(jnp.float32), axis=0)
    d_hidden = back_product(d_ffn, w_down)
    d_hidden_in = (d_hidden * gelu_slope(hidden_in)).astype(jnp.bfloat16)
    grad_up = weight_grad(first_low, d_hidden_in)
    grad_bup = jnp.sum(d_hidden_in.astype(jnp.float32), axis=0)
    d_first = d_ztwo + back_product(d_hidden_in, w_up)
    sink, pull_one = jax.vjp(layer_norm, z_one, gain_one, shift_one)
    d_zone, d_gain_one, d_shift_one = pull_one(d_first)
    d_branch = d_zone.astype(jnp.bfloat16)
    grad_out_w = weight_grad(context_rows, d_branch)
    grad_bout = jnp.sum(d_branch.astype(jnp.float32), axis=0)
    d_context = back_product(d_branch, w_out).astype(jnp.bfloat16).reshape(local_shape)
    d_context_heads = lax.all_to_all(d_context, "head", split_axis=2, concat_axis=1, tiled=True)
    d_context_split = d_context_heads.reshape(split_shape)

    def backward_item(items):
        return attend_backward(items[0], items[1], items[2], items[3], items[4], scale)

    d_query, d_keys, d_values = lax.map(
        backward_item, (q_split, k_split, v_split, d_context_split, log_total)
    )
    joined_shape = (seq_local, length_full, head_local * HD)
    d_query_tok, d_keys_tok, d_values_tok = (
        lax.all_to_all(
            as_sent(d_query.reshape(joined_shape)), "head", split_axis=1, concat_axis=2, tiled=True
        ),
        lax.all_to_all(
            as_sent(d_keys.reshape(joined_shape)), "head", split_axis=1, concat_axis=2, tiled=True
        ),
        lax.all_to_all(
            as_sent(d_values.reshape(joined_shape)), "head", split_axis=1, concat_axis=2, tiled=True
        ),
    )
    d_query_rows = d_query_tok.reshape(seq_local * tok_local, width)
    d_keys_rows = d_keys_tok.reshape(seq_local * tok_local, width)
    d_values_rows = d_values_tok.reshape(seq_local * tok_local, width)
    grad_query = weight_grad(token_rows, d_query_rows)
    grad_key = weight_grad(token_rows, d_keys_rows)
    grad_value = weight_grad(token_rows, d_values_rows)
    grad_bquery = jnp.sum(d_query_rows.astype(jnp.float32), axis=0)
    grad_bvalue = jnp.sum(d_values_rows.astype(jnp.float32), axis=0)
    input_grad = (
        d_zone
        + back_product(d_query_rows, w_query)
        + back_product(d_keys_rows, w_key)
        + back_product(d_values_rows, w_value)
    )
    input_grad = input_grad.reshape(local_shape)
    grad_blocks = join_matrices([grad_query, grad_key, grad_value, grad_out_w, grad_up, grad_down])
    padded = jnp.concatenate(
        [grad_blocks, jnp.zeros((slot_total - grad_blocks.shape[0], BLK, BLK), jnp.float32)], 0
    )
    slot_terms = padded[owner_slot]
    vector_terms = jnp.concatenate(
        [
            grad_bquery,
            grad_bvalue,
            grad_bout,
            d_gain_one,
            d_shift_one,
            grad_bup,
            grad_bdown,
            d_gain_two,
            d_shift_two,
        ],
        0,
    )
    slot_grad, vec_grad = (
        lax.psum_scatter(slot_terms, ("seq", "head"), scatter_dimension=0, tiled=True),
        lax.psum_scatter(vector_terms, ("seq", "head"), scatter_dimension=0, tiled=True),
    )
    first_moment, second_moment, updated = rotate_adam(
        slot_grad, master, moment_one, moment_two, basis_left, basis_right
    )
    correct = 1.0 - 0.5**STEP
    vec_first = 0.5 * vec_moment_one + 0.5 * vec_grad
    vec_second = 0.5 * vec_moment_two + 0.5 * vec_grad * vec_grad
    vec_new = vec_master - VEC_RATE * (vec_first / correct) / (
        jnp.sqrt(vec_second / correct) + ADAM_EPS
    )
    new_average = KEEP * average + (1.0 - KEEP) * updated
    return (
        layer_out,
        input_grad,
        slot_grad,
        vec_grad,
        first_moment,
        second_moment,
        updated,
        updated.astype(jnp.bfloat16),
        new_average,
        vec_first,
        vec_second,
        vec_new,
    )


def solution(mesh):
    placed = (
        P("seq", "head", None),
        P("seq", "head", None),
        P("seq", "head"),
        P("seq", "head"),
        P(),
        P(("seq", "head"), None, None),
        P(("seq", "head"), None, None),
        P(("seq", "head"), None, None),
        P(("seq", "head"), None, None),
        P(("seq", "head"), None, None),
        P(("seq", "head"), None, None),
        P(("seq", "head")),
        P(("seq", "head")),
        P(("seq", "head")),
    )
    return jax.shard_map(
        body,
        mesh=mesh,
        in_specs=placed,
        out_specs=(
            P("seq", "head", None),
            P("seq", "head", None),
            P(("seq", "head"), None, None),
            P(("seq", "head")),
            P(("seq", "head"), None, None),
            P(("seq", "head"), None, None),
            P(("seq", "head"), None, None),
            P(("seq", "head"), None, None),
            P(("seq", "head"), None, None),
            P(("seq", "head")),
            P(("seq", "head")),
            P(("seq", "head")),
        ),
        check_vma=False,
    )
```

profile of v0, /device:TPU:11, one launch (start us, length us, event | category | flops | bytes accessed | tf_op | source)
XLA Modules:
  0.0 633.9 jit_solution(15977619600493150822)
XLA Ops:
  12.7 40.3 %all-reduce = f32[6144]{0:T(1024)S(1)} all-reduce(f32[6144]{0:T(1024)S(1)} %dynamic-update-slice), channel_id=1, replica_groups=mesh['seq'=8,'head'=4] {'seq','head'}, use_global_device_ids=true, to_apply=%add | all-reduce | flops 6144 | bytes 49152
  53.0 37.2 %all-gather.2.cloned.1.call-done = bf16[256,128,128]{2,1,0:T(8,128)(2,1)} async-done(((bf16[8,128,128]{2,1,0:T(8,128)(2,1)}), bf16[256,128,128]{2,1,0:T(8,128)(2,1)}) %all-gather.2.cloned.1.call-update) | async-done | bytes 8388624 | tf_op jit(solution)/shard_map/all_gather | solution.py:212
  90.2 11.5 %gather_fusion = bf16[192,128,128]{2,1,0:T(8,128)(2,1)} fusion(bf16[256,128,128]{2,1,0:T(8,128)(2,1)} %all-gather.2.cloned.1.call-done, s32[1024]{0:T(1024)S(1)} %pad_clamp_fusion.1), kind=kCustom, calls=%fused_computation | custom fusion | bytes 12583680 | tf_op jit(solution)/shard_map/gather | solution.py:221
  109.7 3.7 all-to-all-start
  120.1 6.8 %all-to-all-done = bf16[3,256,512]{1,0,2:T(4,128)(2,1)S(1)} async-done(((bf16[3,256,512]{1,0,2:T(4,128)(2,1)}), bf16[3,256,512]{1,0,2:T(4,128)(2,1)S(1)}, u32[]{:S(2)}, u32[]{:S(2)}) %all-to-all-start) | async-done | bytes 786464 | tf_op jit(solution)/shard_map/all_to_all | solution.py:249
  127.0 4.5 all-to-all-start.1
  138.1 6.8 %all-to-all-done.1 = bf16[3,256,512]{1,0,2:T(4,128)(2,1)S(1)} async-done(((bf16[3,256,512]{1,0,2:T(4,128)(2,1)}), bf16[3,256,512]{1,0,2:T(4,128)(2,1)S(1)}, u32[]{:S(2)}, u32[]{:S(2)}) %all-to-all-start.1) | async-done | bytes 786464 | tf_op jit(solution)/shard_map/all_to_all | solution.py:247
  144.9 5.4 all-to-all-start.2
  156.6 7.2 %all-to-all-done.2 = bf16[3,256,512]{1,0,2:T(4,128)(2,1)} async-done(((bf16[3,256,512]{1,0,2:T(4,128)(2,1)}), bf16[3,256,512]{1,0,2:T(4,128)(2,1)}, u32[]{:S(2)}, u32[]{:S(2)}) %all-to-all-start.2) | async-done | bytes 786464 | tf_op jit(solution)/shard_map/all_to_all | solution.py:248
  169.4 19.9 %while.26 = (s32[]{:T(128)}, bf16[3,1024,2,64]{1,3,2,0:T(8,128)(2,1)}, f32[3,2,1024,1]{2,1,3,0:T(2,128)S(1)}, bf16[3,1024,2,64]{1,3,2,0:T(8,128)(2,1)S(1)}, bf16...) while((s32[]{:T(128)}, ...), condition=%wide.region_6.7_spmd, body=%wide.region_1.6_spmd.sunk | while | flops 556400640 | bytes 27347584 | solution.py:262
  192.0 5.4 all-to-all-start.3
  197.5 3.1 fusion.151
  200.6 4.8 fusion.168
  205.4 4.5 copy.133
  209.9 4.3 copy.132
  227.3 5.5 convert_reduce_fusion
  241.2 3.5 all-to-all-start.4
  244.7 13.5 %all-to-all-done.4 = bf16[3,256,512]{1,0,2:T(4,128)(2,1)S(1)} async-done(((bf16[3,256,512]{1,0,2:T(4,128)(2,1)}), bf16[3,256,512]{1,0,2:T(4,128)(2,1)S(1)}, u32[]{:S(2)}, u32[]{:S(2)}) %all-to-all-start.4) | async-done | bytes 786464 | tf_op jit(solution)/shard_map/all_to_all | solution.py:297
  264.6 38.8 %while.27 = (s32[]{:T(128)}, bf16[3,1024,2,64]{1,3,2,0:T(8,128)(2,1)}, bf16[3,1024,2,64]{1,3,2,0:T(8,128)(2,1)}, bf16[3,1024,2,64]{1,3,2,0:T(8,128)(2,1)}, bf16[...) while((s32[]{:T(128)}, ...), condition=%wide.region_18.19_spmd, body=%wide.region_15.18_spmd.sunk | while | flops 1368782848 | bytes 72171200 | solution.py:303
  305.8 4.6 all-to-all-start.5
  311.9 12.0 %all-to-all-done.5 = bf16[3,1024,128]{2,0,1:T(4,128)(2,1)S(1)} async-done(((bf16[3,1024,128]{2,0,1:T(4,128)(2,1)}), bf16[3,1024,128]{2,0,1:T(4,128)(2,1)S(1)}, u32[]{:S(2)}, u32[]{:S(2)}) %all-to-all-start.5) | async-done | bytes 786464 | tf_op jit(solution)/shard_map/all_to_all | solution.py:308
  323.9 5.4 all-to-all-start.7
  329.3 5.8 fusion.174
  340.7 5.8 convolution_bitcast_fusion
  349.0 4.2 all-to-all-start.6
  355.0 3.1 copy.172
  358.1 3.2 copy.150
  361.3 5.5 reshape.424
  366.8 4.8 copy.151
  416.5 17.7 %gather_fusion.1 = f32[256,128,128]{2,1,0:T(8,128)} fusion(f32[256,128,128]{2,1,0:T(8,128)} %broadcast_dynamic-update-slice_fusion, s32[1024]{0:T(1024)S(1)} %pad_clamp_fusion), kind=kCustom, calls=%fused_computation.1 | custom fusion | bytes 33555456 | tf_op jit(solution)/shard_map/gather | solution.py:337
  434.9 46.8 %all-reduce.1 = f32[6144]{0:T(1024)S(1)} all-reduce(f32[6144]{0:T(1024)S(1)} %constant_dynamic-update-slice_fusion.7), channel_id=3, replica_groups=mesh['seq'=8,'head'=4] {'seq','head'}, use_global_device_ids=true, to_apply=%region_29.30.clone | all-reduce | flops 6144 | bytes 49152
  487.9 131.4 %reduce-scatter.2.cloned.1.call-done = f32[8,128,128]{2,1,0:T(8,128)} async-done(((f32[256,128,128]{2,1,0:T(8,128)}), f32[8,128,128]{2,1,0:T(8,128)}) %reduce-scatter.2.cloned.1.call-update) | async-done | bytes 524304 | tf_op jit(solution)/shard_map/reduce_scatter | solution.py:353
  (313 shorter events, 200.3 us)
Async XLA Ops:
  7.2 614.3 %copy-start = (f32[8,128,128]{2,1,0:T(8,128)S(1)}, f32[8,128,128]{2,1,0:T(8,128)}, u32[]{:S(2)}) copy-start(f32[8,128,128]{2,1,0:T(8,128)} %param.27) | copy-start | bytes 1572868
  7.2 83.0 %all-gather.2.cloned.1.call-start = ((), (), s32[]{:S(2)}) async-start(), calls=%async_computation.9 | async-start | bytes 8650752 | tf_op jit(solution)/shard_map/all_gather | solution.py:212
  109.7 17.2 %all-to-all-start = ((bf16[3,256,512]{1,0,2:T(4,128)(2,1)}), bf16[3,256,512]{1,0,2:T(4,128)(2,1)S(1)}, u32[]{:S(2)}, u32[]{:S(2)}) async-start(bf16[3,256,512]{1,0,2:T(4,128)(2,1)} %copy.118), calls=%async_computation | async-start | bytes 2097152 | tf_op jit(solution)/shard_map/all_to_all | solution.py:249
  127.0 17.9 %all-to-all-start.1 = ((bf16[3,256,512]{1,0,2:T(4,128)(2,1)}), bf16[3,256,512]{1,0,2:T(4,128)(2,1)S(1)}, u32[]{:S(2)}, u32[]{:S(2)}) async-start(bf16[3,256,512]{1,0,2:T(4,128)(2,1)} %copy.122), calls=%async_computation.1 | async-start | bytes 2097152 | tf_op jit(solution)/shard_map/all_to_all | solution.py:247
  135.3 15.0 %copy-start.50 = (s32[3,16]{1,0:T(4,128)S(1)}, s32[3,16]{1,0:T(4,128)}, u32[]{:S(2)}) copy-start(s32[3,16]{1,0:T(4,128)} %param.20) | copy-start | bytes 580
  135.3 15.2 %copy-start.51 = (s32[3,16]{1,0:T(4,128)S(1)}, s32[3,16]{1,0:T(4,128)}, u32[]{:S(2)}) copy-start(s32[3,16]{1,0:T(4,128)} %param.21) | copy-start | bytes 580
  144.9 18.9 %all-to-all-start.2 = ((bf16[3,256,512]{1,0,2:T(4,128)(2,1)}), bf16[3,256,512]{1,0,2:T(4,128)(2,1)}, u32[]{:S(2)}, u32[]{:S(2)}) async-start(bf16[3,256,512]{1,0,2:T(4,128)(2,1)} %copy.126), calls=%async_computation.2 | async-start | bytes 2097152 | tf_op jit(solution)/shard_map/all_to_all | solution.py:248
  189.4 11.2 %copy-start.3 = (bf16[3,1024,2,64]{1,3,2,0:T(8,128)(2,1)}, bf16[3,1024,2,64]{1,3,2,0:T(8,128)(2,1)S(1)}, u32[]{:S(2)}) copy-start(bf16[3,1024,2,64]{1,3,2,0:T(8,128)(2,1)S(1)} %get-tuple-element.380) | copy-start | bytes 2359300
  192.0 22.6 %all-to-all-start.3 = ((bf16[3,1024,128]{2,0,1:T(4,128)(2,1)}), bf16[3,1024,128]{2,0,1:T(4,128)(2,1)}, u32[]{:S(2)}, u32[]{:S(2)}) async-start(bf16[3,1024,128]{2,0,1:T(4,128)(2,1)} %copy.128), calls=%async_computation.3 | async-start | bytes 2097152 | tf_op jit(solution)/shard_map/all_to_all | solution.py:264
  218.2 17.5 %copy-start.8 = (f32[768,512]{1,0:T(8,128)}, f32[768,512]{1,0:T(8,128)S(1)}, u32[]{:S(2)}) copy-start(f32[768,512]{1,0:T(8,128)S(1)} %get-tuple-element.182) | copy-start | bytes 4718596
  241.2 17.0 %all-to-all-start.4 = ((bf16[3,256,512]{1,0,2:T(4,128)(2,1)}), bf16[3,256,512]{1,0,2:T(4,128)(2,1)S(1)}, u32[]{:S(2)}, u32[]{:S(2)}) async-start(bf16[3,256,512]{1,0,2:T(4,128)(2,1)} %copy.134), calls=%async_computation.4 | async-start | bytes 2097152 | tf_op jit(solution)/shard_map/all_to_all | solution.py:297
  303.4 7.0 %copy-start.47 = (s32[256]{0:T(256)S(1)}, s32[256]{0:T(256)}, u32[]{:S(2)}) copy-start(s32[256]{0:T(256)} %copy-done.46) | copy-start | bytes 3076
  303.4 7.0 %copy-start.18 = (bf16[3,1024,2,64]{1,3,2,0:T(8,128)(2,1)S(1)}, bf16[3,1024,2,64]{1,3,2,0:T(8,128)(2,1)}, u32[]{:S(2)}) copy-start(bf16[3,1024,2,64]{1,3,2,0:T(8,128)(2,1)} %get-tuple-element.98) | copy-start | bytes 2359300
  305.8 23.4 %copy-start.33 = (bf16[768,512]{1,0:T(8,128)(2,1)S(1)}, bf16[768,512]{1,0:T(8,128)(2,1)}, u32[]{:S(2)}) copy-start(bf16[768,512]{1,0:T(8,128)(2,1)} %copy-done.32) | copy-start | bytes 2359300
  305.8 18.0 %all-to-all-start.5 = ((bf16[3,1024,128]{2,0,1:T(4,128)(2,1)}), bf16[3,1024,128]{2,0,1:T(4,128)(2,1)S(1)}, u32[]{:S(2)}, u32[]{:S(2)}) async-start(bf16[3,1024,128]{2,0,1:T(4,128)(2,1)} %copy.136), calls=%async_computation.5 | async-start | bytes 2097152 | tf_op jit(solution)/shard_map/all_to_all | solution.py:308
  323.9 25.1 %all-to-all-start.7 = ((bf16[3,1024,128]{2,0,1:T(4,128)(2,1)}), bf16[3,1024,128]{2,0,1:T(4,128)(2,1)}, u32[]{:S(2)}, u32[]{:S(2)}) async-start(bf16[3,1024,128]{2,0,1:T(4,128)(2,1)} %copy.142), calls=%async_computation.7 | async-start | bytes 2097152 | tf_op jit(solution)/shard_map/all_to_all | solution.py:314
  346.5 6.8 %copy-start.22 = (bf16[512,768]{1,0:T(8,128)(2,1)S(1)}, bf16[512,768]{1,0:T(8,128)(2,1)}, u32[]{:S(2)}) copy-start(bf16[512,768]{1,0:T(8,128)(2,1)} %copy.148) | copy-start | bytes 2359300
  346.5 6.8 %copy-start.23 = (bf16[512,768]{1,0:T(8,128)(2,1)S(1)}, bf16[512,768]{1,0:T(8,128)(2,1)}, u32[]{:S(2)}) copy-start(bf16[512,768]{1,0:T(8,128)(2,1)} %copy.161) | copy-start | bytes 2359300
  349.0 41.2 %all-to-all-start.6 = ((bf16[3,1024,128]{2,0,1:T(4,128)(2,1)}), bf16[3,1024,128]{2,0,1:T(4,128)(2,1)}, u32[]{:S(2)}, u32[]{:S(2)}) async-start(bf16[3,1024,128]{2,0,1:T(4,128)(2,1)} %copy.139), calls=%async_computation.6 | async-start | bytes 2097152 | tf_op jit(solution)/shard_map/all_to_all | solution.py:311
  353.3 266.1 %reduce-scatter.2.cloned.1.call-start = ((), (), s32[]{:S(2)}) async-start(), calls=%async_computation.10 | async-start | bytes 17301504 | tf_op jit(solution)/shard_map/reduce_scatter | solution.py:353
  375.2 6.8 %copy-start.13 = (bf16[3,256,4,128]{3,2,1,0:T(4,128)(2,1)}, bf16[3,256,4,128]{3,2,1,0:T(4,128)(2,1)S(1)}, u32[]{:S(2)}) copy-start(bf16[3,256,4,128]{3,2,1,0:T(4,128)(2,1)S(1)} %copy.144) | copy-start | bytes 2359300
  400.9 6.0 copy-start.11
  434.2 47.6 %copy-start.45 = (f32[192]{0:T(256)S(1)}, f32[192]{0:T(256)}, u32[]{:S(2)}) copy-start(f32[192]{0:T(256)} %param.29) | copy-start | bytes 2308
  434.2 47.6 %copy-start.52 = (f32[192]{0:T(256)S(1)}, f32[192]{0:T(256)}, u32[]{:S(2)}) copy-start(f32[192]{0:T(256)} %param.31) | copy-start | bytes 2308
  434.2 47.6 %copy-start.53 = (f32[192]{0:T(256)S(1)}, f32[192]{0:T(256)}, u32[]{:S(2)}) copy-start(f32[192]{0:T(256)} %param.30) | copy-start | bytes 2308
  434.4 51.7 %copy-start.7 = (f32[768,512]{1,0:T(8,128)S(1)}, f32[768,512]{1,0:T(8,128)}, u32[]{:S(2)}) copy-start(f32[768,512]{1,0:T(8,128)} %copy-done.6) | copy-start | bytes 4718596
  434.4 51.7 %copy-start.25 = (bf16[4,4,128,128]{3,1,2,0:T(4,128)(2,1)S(1)}, bf16[4,4,128,128]{3,1,2,0:T(4,128)(2,1)}, u32[]{:S(2)}) copy-start(bf16[4,4,128,128]{3,1,2,0:T(4,128)(2,1)} %copy-done.24) | copy-start | bytes 1572868
  434.4 51.7 %copy-start.39 = (f32[768]{0:T(1024)S(1)}, f32[768]{0:T(1024)}, u32[]{:S(2)}) copy-start(f32[768]{0:T(1024)} %copy-done.38) | copy-start | bytes 9220
  434.6 51.5 %copy-start.14 = (bf16[3,256,4,128]{3,2,1,0:T(4,128)(2,1)S(1)}, bf16[3,256,4,128]{3,2,1,0:T(4,128)(2,1)}, u32[]{:S(2)}) copy-start(bf16[3,256,4,128]{3,2,1,0:T(4,128)(2,1)} %copy-done.13) | copy-start | bytes 2359300
  487.9 135.6 %copy-start.34 = (f32[8,128,128]{2,1,0:T(8,128)S(1)}, f32[8,128,128]{2,1,0:T(8,128)}, u32[]{:S(2)}) copy-start(f32[8,128,128]{2,1,0:T(8,128)} %param.26) | copy-start | bytes 1572868
  487.9 136.5 %copy-start.28 = (f32[8,128,128]{2,1,0:T(8,128)S(1)}, f32[8,128,128]{2,1,0:T(8,128)}, u32[]{:S(2)}) copy-start(f32[8,128,128]{2,1,0:T(8,128)} %param.23) | copy-start | bytes 1572868
  487.9 136.5 %copy-start.35 = (f32[8,128,128]{2,1,0:T(8,128)S(1)}, f32[8,128,128]{2,1,0:T(8,128)}, u32[]{:S(2)}) copy-start(f32[8,128,128]{2,1,0:T(8,128)} %param.28) | copy-start | bytes 1572868
  (38 other events, 93.6 us)
Sparse Core Ops, SparseCore 0:
  11.4 78.6 all-gather.1
  434.4 184.8 reduce-scatter.1
where the time goes:
time: 645 us; the launch traced here: 634 us
  waiting for transfers between devices  215 us (33%)
  local copies, waits for them, and re-layouts  155 us (24%)
  matrix products  96.7 us (15%)
  blocking collectives  87.1 us (14%)
  starting transfers between devices  36.8 us (6%)
  other arithmetic  28.5 us (4%)
  between operations  15.2 us (2%)
    reduce_scatter x1, waiting for transfers between devices, body(): lax.psum_scatter(slot_terms, ('seq', 'head'), scatter_dimension=0, tiled=...  131 us
    unnamed x2, blocking collectives  87.1 us
    all_gather x1, waiting for transfers between devices, body(): lax.all_gather(master, ('seq', 'head'), axis=0, tiled=True)  37.2 us
    reshape x9, local copies, waits for them, and re-layouts, join_matrices(): matrix.reshape(row_count, BLK, col_count, BLK).transpose(0, 2, 1, 3)  29 us
    unnamed x132, local copies, waits for them, and re-layouts  25.3 us
    dot_general x6, matrix products, weight_grad(): jnp.einsum('ti,to->io', left, right, preferred_element_type=jnp.float32)  20.6 us
    gather x1, local copies, waits for them, and re-layouts, body(): slot_terms = padded[owner_slot]  17.7 us
    dot_general x6, matrix products, back_product(): jnp.einsum('to,io->ti', grads, weight, preferred_element_type=jnp.float32)  14.4 us
  transfers between devices with their start and end apart: 10, of which 7 were waited for; matrix products, arithmetic and copies ran while one was open for 16% of the time, Pallas kernels for 0%

commit v1 on v0

--- a/solution.py
+++ b/solution.py
@@ -1,8 +1,11 @@
+import functools
 import math
 
 import jax
 import jax.numpy as jnp
 from jax import lax
+from jax.experimental import pallas as pl
+from jax.experimental.pallas import tpu as pltpu
 from jax.sharding import PartitionSpec as P
 
 D = 512
@@ -190,6 +193,469 @@
 
 def back_product(grads, weight):
     return jnp.einsum("to,io->ti", grads, weight, preferred_element_type=jnp.float32)
+
+
+MESH = pl.DeviceIdType.MESH
+VEC_ROWS = 16
+
+
+def cut(seq_size, head_size):
+    cores = 2 if head_size % 2 == 0 else 1
+    rows = 1
+    while 2 * (rows * 2) ** 2 <= seq_size and seq_size % (rows * 2) == 0:
+        rows = rows * 2
+    return (seq_size // rows, rows, head_size // cores, cores)
+
+
+def place(dims):
+    size_z, size_x, size_y, size_c = dims
+    seq = lax.axis_index("seq")
+    head = lax.axis_index("head")
+    return (
+        lax.div(seq, size_x),
+        lax.rem(seq, size_x),
+        lax.div(head, size_c),
+        lax.rem(head, size_c),
+    )
+
+
+def device(dims, coords):
+    return (coords[0] * dims[1] + coords[1], coords[2] * dims[3] + coords[3])
+
+
+def flat(dims, coords):
+    return ((coords[0] * dims[1] + coords[1]) * dims[2] + coords[2]) * dims[3] + coords[3]
+
+
+def moved(dims, coords, axis, step):
+    new = list(coords)
+    new[axis] = lax.rem(coords[axis] + step, dims[axis])
+    return tuple(new)
+
+
+def greet(dims, coords):
+    barrier = pltpu.get_barrier_semaphore()
+    count = 0
+    for axis in range(4):
+        for step in range(1, dims[axis]):
+            pl.semaphore_signal(
+                barrier,
+                inc=1,
+                device_id=device(dims, moved(dims, coords, axis, step)),
+                device_id_type=MESH,
+            )
+            count = count + 1
+    pl.semaphore_wait(barrier, count)
+
+
+def greet_head(head_size):
+    barrier = pltpu.get_barrier_semaphore()
+    seq = lax.axis_index("seq")
+    head = lax.axis_index("head")
+    for step in range(1, head_size):
+        pl.semaphore_signal(
+            barrier, inc=1, device_id=(seq, lax.rem(head + step, head_size)), device_id_type=MESH
+        )
+    pl.semaphore_wait(barrier, head_size - 1)
+
+
+def gather_kernel(
+    dims, x_ref, w_ref, xf_ref, wf_ref, own_sem, x_send, x_recv, w_send, w_recv
+):
+    me = place(dims)
+    size_z, size_x, size_y, size_c = dims
+    head_me = me[2] * size_c + me[3]
+    own_x = pltpu.make_async_copy(x_ref, xf_ref.at[:, head_me], own_sem.at[0])
+    own_w = pltpu.make_async_copy(w_ref, wf_ref.at[flat(dims, me)], own_sem.at[1])
+    own_x.start()
+    own_w.start()
+    greet(dims, me)
+    started = []
+
+    def send_x(source, head, target, number):
+        copy = pltpu.make_async_remote_copy(
+            src_ref=source,
+            dst_ref=xf_ref.at[:, head],
+            send_sem=x_send.at[number],
+            recv_sem=x_recv.at[head],
+            device_id=device(dims, target),
+            device_id_type=MESH,
+        )
+        copy.start()
+        started.append(copy)
+
+    def arrived_x(head):
+        pltpu.make_async_remote_copy(
+            src_ref=x_ref,
+            dst_ref=xf_ref.at[:, head],
+            send_sem=x_send.at[0],
+            recv_sem=x_recv.at[head],
+            device_id=device(dims, me),
+            device_id_type=MESH,
+        ).wait_recv()
+
+    count = [0]
+
+    def send_w(source, index, target):
+        number = count[0]
+        count[0] = number + 1
+        copy = pltpu.make_async_remote_copy(
+            src_ref=source,
+            dst_ref=wf_ref.at[index],
+            send_sem=w_send.at[number],
+            recv_sem=w_recv.at[index],
+            device_id=device(dims, target),
+            device_id_type=MESH,
+        )
+        copy.start()
+        started.append(copy)
+
+    def arrived_w(index):
+        pltpu.make_async_remote_copy(
+            src_ref=w_ref,
+            dst_ref=wf_ref.at[index],
+            send_sem=w_send.at[0],
+            recv_sem=w_recv.at[index],
+            device_id=device(dims, me),
+            device_id_type=MESH,
+        ).wait_recv()
+
+    order = [0, 2, 1, 3]
+
+    def forward(source, coords, after):
+        for axis in order[after:]:
+            for step in range(1, dims[axis]):
+                send_w(source, flat(dims, coords), moved(dims, me, axis, step))
+
+    number = 0
+    for step in range(1, size_y):
+        send_x(x_ref, head_me, moved(dims, me, 2, step), number)
+        number = number + 1
+    for step in range(1, size_c):
+        send_x(x_ref, head_me, moved(dims, me, 3, step), number)
+        number = number + 1
+    forward(w_ref, me, 0)
+    held = [me]
+    for level in range(3):
+        axis = order[level]
+        fresh = []
+        for step in range(1, dims[axis]):
+            for coords in held:
+                source = moved(dims, coords, axis, step)
+                arrived_w(flat(dims, source))
+                forward(wf_ref.at[flat(dims, source)], source, level + 1)
+                fresh.append(source)
+        held = held + fresh
+        if level == 1:
+            for step in range(1, size_y):
+                other = moved(dims, me, 2, step)
+                head = other[2] * size_c + other[3]
+                arrived_x(head)
+                for hop in range(1, size_c):
+                    send_x(xf_ref.at[:, head], head, moved(dims, me, 3, hop), number)
+                    number = number + 1
+    for step in range(1, size_c):
+        for coords in held:
+            arrived_w(flat(dims, moved(dims, coords, 3, step)))
+        for across in range(size_y):
+            other = moved(dims, moved(dims, me, 3, step), 2, across)
+            arrived_x(other[2] * size_c + other[3])
+    for copy in started:
+        copy.wait_send()
+    own_x.wait()
+    own_w.wait()
+
+
+def gather_all(dims, inputs, packed):
+    size_z, size_x, size_y, size_c = dims
+    total = size_z * size_x * size_y * size_c
+    head_size = size_y * size_c
+    seq_local, tok_local, width = inputs.shape
+    any_space = pl.BlockSpec(memory_space=pl.ANY)
+    whole = pl.BlockSpec(memory_space=pltpu.VMEM)
+    sends_x = (size_y - 1) * size_c + size_c - 1
+    sends_w = (
+        (size_z - 1)
+        + size_z * (size_y - 1)
+        + size_z * size_y * (size_x - 1)
+        + size_z * size_y * size_x * (size_c - 1)
+    )
+    return pl.pallas_call(
+        functools.partial(gather_kernel, dims),
+        out_shape=(
+            jax.ShapeDtypeStruct((seq_local, head_size, tok_local, width), inputs.dtype),
+            jax.ShapeDtypeStruct((total,) + packed.shape, packed.dtype),
+        ),
+        in_specs=[whole, whole],
+        out_specs=(any_space, any_space),
+        scratch_shapes=[
+            pltpu.SemaphoreType.DMA((2,)),
+            pltpu.SemaphoreType.DMA((max(sends_x, 1),)),
+            pltpu.SemaphoreType.DMA((head_size,)),
+            pltpu.SemaphoreType.DMA((max(sends_w, 1),)),
+            pltpu.SemaphoreType.DMA((total,)),
+        ],
+        compiler_params=pltpu.CompilerParams(collective_id=0, has_side_effects=True),
+        name="gather_all",
+    )(inputs, packed)
+
+
+def exchange_kernel(head_size, src_ref, dst_ref, own_sem, send_sem, recv_sem):
+    seq = lax.axis_index("seq")
+    head = lax.axis_index("head")
+    own = pltpu.make_async_copy(src_ref.at[head], dst_ref.at[head], own_sem)
+    own.start()
+    greet_head(head_size)
+    copies = []
+    for step in [2, 1, 3] if head_size == 4 else range(1, head_size):
+        peer = lax.rem(head + step, head_size)
+        copy = pltpu.make_async_remote_copy(
+            src_ref=src_ref.at[peer],
+            dst_ref=dst_ref.at[head],
+            send_sem=send_sem.at[step],
+            recv_sem=recv_sem.at[step],
+            device_id=(seq, peer),
+            device_id_type=MESH,
+        )
+        copy.start()
+        copies.append(copy)
+    for copy in copies:
+        copy.wait()
+    own.wait()
+
+
+def exchange(array, number):
+    head_size = array.shape[0]
+    if head_size == 1:
+        return array
+    whole = pl.BlockSpec(memory_space=pltpu.VMEM)
+    return pl.pallas_call(
+        functools.partial(exchange_kernel, head_size),
+        out_shape=jax.ShapeDtypeStruct(array.shape, array.dtype),
+        in_specs=[whole],
+        out_specs=whole,
+        scratch_shapes=[
+            pltpu.SemaphoreType.DMA,
+            pltpu.SemaphoreType.DMA((head_size,)),
+            pltpu.SemaphoreType.DMA((head_size,)),
+        ],
+        compiler_params=pltpu.CompilerParams(collective_id=number, has_side_effects=True),
+        name="exchange",
+    )(array)
+
+
+def scatter_kernel(
+    dims,
+    slots,
+    owner_ref,
+    blocks_ref,
+    vec_ref,
+    grad_ref,
+    vec_out_ref,
+    term,
+    got_c,
+    got_x,
+    got_y,
+    got_z,
+    send_c,
+    send_x,
+    send_y,
+    send_z,
+    recv_c,
+    recv_x,
+    recv_y,
+    recv_z,
+):
+    me = place(dims)
+    size_z, size_x, size_y, size_c = dims
+    rows = slots * BLK
+    greet(dims, me)
+
+    def block_of(dest, slot):
+        owner = owner_ref[dest * slots + slot]
+        block = blocks_ref[jnp.minimum(owner, NBLK - 1)]
+        return jnp.where(owner < NBLK, block, jnp.zeros_like(block))
+
+    def total_of(dest, extras, keep_block, keep_vec):
+        def one(slot, carry):
+            value = block_of(dest, slot).astype(jnp.float32)
+            span = pl.ds(pl.multiple_of(slot * BLK, BLK), BLK)
+            for ref, lead in extras:
+                value = value + ref[lead + (span,)].astype(jnp.float32)
+            keep_block(slot, span, value)
+            return carry
+
+        lax.fori_loop(0, slots, one, 0)
+        value = vec_ref[dest].astype(jnp.float32)
+        for ref, lead in extras:
+            value = value + ref[lead + (pl.ds(rows, VEC_ROWS),)].astype(jnp.float32)
+        keep_vec(value)
+
+    def into_term(dest, extras):
+        def keep_block(slot, span, value):
+            term[dest, span] = value.astype(jnp.bfloat16)
+
+        def keep_vec(value):
+            term[dest, pl.ds(rows, VEC_ROWS)] = value.astype(jnp.bfloat16)
+
+        total_of(dest, extras, keep_block, keep_vec)
+
+    def remote(dest, got, send, recv, hop, index, target):
+        return pltpu.make_async_remote_copy(
+            src_ref=term.at[dest],
+            dst_ref=got.at[hop, index],
+            send_sem=send.at[hop, index],
+            recv_sem=recv.at[hop, index],
+            device_id=device(dims, target),
+            device_id_type=MESH,
+        )
+
+    def each(axis, count, coords_of, extras_of, got, send, recv):
+        for step in range(1, dims[axis]):
+            target = moved(dims, me, axis, step)
+
+            def one(index, carry, step=step, target=target):
+                coords = list(coords_of(index))
+                coords[axis] = target[axis]
+                dest = flat(dims, coords)
+                into_term(dest, extras_of(coords))
+                remote(dest, got, send, recv, step - 1, index, target).start()
+                return carry
+
+            lax.fori_loop(0, count, one, 0)
+
+    def wait_for(axis, got, send, recv, index):
+        found = []
+        for step in range(1, dims[axis]):
+            remote(0, got, send, recv, step - 1, index, moved(dims, me, axis, step)).wait_recv()
+            found.append((got, (step - 1, index)))
+        return found
+
+    def index_c(coords):
+        away = lax.rem(coords[1] - me[1] + size_x, size_x)
+        order = lax.rem(away + size_x - 1, size_x)
+        return (order * size_z + coords[0]) * size_y + coords[2]
+
+    def coords_c(index):
+        order = lax.div(index, size_z * size_y)
+        rest = lax.rem(index, size_z * size_y)
+        x = lax.rem(me[1] + 1 + order, size_x)
+        return (lax.div(rest, size_y), x, lax.rem(rest, size_y), me[3])
+
+    def coords_x(index):
+        return (lax.div(index, size_y), me[1], lax.rem(index, size_y), me[3])
+
+    def coords_y(index):
+        return (index, me[1], me[2], me[3])
+
+    def coords_z(index):
+        return me
+
+    def extras_c(coords):
+        return []
+
+    def extras_x(coords):
+        return wait_for(3, got_c, send_c, recv_c, index_c(coords))
+
+    def extras_y(coords):
+        return extras_x(coords) + wait_for(
+            1, got_x, send_x, recv_x, coords[0] * size_y + coords[2]
+        )
+
+    def extras_z(coords):
+        return extras_y(coords) + wait_for(2, got_y, send_y, recv_y, coords[0])
+
+    each(3, size_z * size_x * size_y, coords_c, extras_c, got_c, send_c, recv_c)
+    each(1, size_z * size_y, coords_x, extras_x, got_x, send_x, recv_x)
+    each(2, size_z, coords_y, extras_y, got_y, send_y, recv_y)
+    each(0, 1, coords_z, extras_z, got_z, send_z, recv_z)
+    extras = extras_z(me) + wait_for(0, got_z, send_z, recv_z, 0)
+
+    def keep_block(slot, span, value):
+        grad_ref[slot] = value
+
+    def keep_vec(value):
+        vec_out_ref[...] = value
+
+    total_of(flat(dims, me), extras, keep_block, keep_vec)
+
+    def drain(axis, count, got, send, recv):
+        for step in range(1, dims[axis]):
+
+            def one(index, carry, step=step):
+                remote(
+                    0, got, send, recv, step - 1, index, moved(dims, me, axis, step)
+                ).wait_send()
+                return carry
+
+            lax.fori_loop(0, count, one, 0)
+
+    drain(3, size_z * size_x * size_y, got_c, send_c, recv_c)
+    drain(1, size_z * size_y, got_x, send_x, recv_x)
+    drain(2, size_z, got_y, send_y, recv_y)
+    drain(0, 1, got_z, send_z, recv_z)
+
+
+def scatter_sums(dims, owner_slot, blocks, vec_terms):
+    size_z, size_x, size_y, size_c = dims
+    total = size_z * size_x * size_y * size_c
+    slots = owner_slot.shape[0] // total
+    chunk = (slots * BLK + VEC_ROWS, BLK)
+    shapes = [
+        (max(size_c - 1, 1), size_z * size_x * size_y),
+        (max(size_x - 1, 1), size_z * size_y),
+        (max(size_y - 1, 1), size_z),
+        (max(size_z - 1, 1), 1),
+    ]
+    whole = pl.BlockSpec(memory_space=pltpu.VMEM)
+    return pl.pallas_call(
+        functools.partial(scatter_kernel, dims, slots),
+        out_shape=(
+            jax.ShapeDtypeStruct((slots, BLK, BLK), jnp.float32),
+            jax.ShapeDtypeStruct((VEC_ROWS, BLK), jnp.float32),
+        ),
+        in_specs=[pl.BlockSpec(memory_space=pltpu.SMEM), whole, whole],
+        out_specs=(whole, whole),
+        scratch_shapes=[pltpu.VMEM((total,) + chunk, jnp.bfloat16)]
+        + [pltpu.VMEM(shape + chunk, jnp.bfloat16) for shape in shapes]
+        + [pltpu.SemaphoreType.DMA(shape) for shape in shapes]
+        + [pltpu.SemaphoreType.DMA(shape) for shape in shapes],
+        compiler_params=pltpu.CompilerParams(
+            collective_id=1, has_side_effects=True, vmem_limit_bytes=60 * 1024 * 1024
+        ),
+        name="scatter_sums",
+    )(owner_slot, blocks, vec_terms)
+
+
+def three_parts(values):
+    high = lax.reduce_precision(values, 8, 7)
+    rest = values - high
+    middle = lax.reduce_precision(rest, 8, 7)
+    low = lax.reduce_precision(rest - middle, 8, 7)
+    return [part.astype(jnp.bfloat16) for part in (high, middle, low)]
+
+
+def as_rows(vector, rows):
+    return jnp.pad(vector, (0, rows * BLK - vector.shape[0])).reshape(rows, BLK)
+
+
+def ceil_to(value, unit):
+    return -(-value // unit) * unit
+
+
+def to_tokens(array, head_size, number, parts=1):
+    seq_local, length, columns = array.shape
+    tokens = length // head_size
+    array = array.reshape(seq_local, head_size, tokens, columns).transpose(1, 0, 2, 3)
+    got = exchange(array, number).reshape(head_size, seq_local * tokens, parts, columns // parts)
+    return got.transpose(1, 2, 0, 3).reshape(seq_local * tokens, head_size * columns)
+
+
+def to_heads(rows, seq_local, head_size, number):
+    columns = rows.shape[1] // head_size
+    array = rows.reshape(seq_local, rows.shape[0] // seq_local, head_size, columns)
+    got = exchange(array.transpose(2, 0, 1, 3), number)
+    return got.transpose(1, 0, 2, 3).reshape(seq_local, -1, columns)
 
 
 def body(
@@ -208,63 +674,71 @@
     vec_moment_one,
     vec_moment_two,
 ):
-    all_slots, all_vector = (
-        lax.all_gather(master, ("seq", "head"), axis=0, tiled=True),
-        lax.all_gather(vec_master, ("seq", "head"), axis=0, tiled=True),
-    )
-    slot_total = all_slots.shape[0]
+    both = ("seq", "head")
+    seq_size = lax.axis_size("seq")
+    head_size = lax.axis_size("head")
+    total = seq_size * head_size
+    head_index = lax.axis_index("head")
+    seq_local, tok_local, width = inputs.shape
+    slots_local = master.shape[0]
+    slot_total = slots_local * total
+    vec_local = vec_master.shape[0]
+
+    dims = cut(seq_size, head_size)
+
+    packed = jnp.concatenate(
+        [
+            master.astype(jnp.bfloat16).reshape(slots_local * BLK, BLK),
+            as_rows(jnp.concatenate(three_parts(vec_master)), VEC_ROWS),
+        ],
+        0,
+    )
+    inputs_full, gathered = gather_all(dims, inputs, packed)
+    all_slots = gathered[:, : slots_local * BLK].reshape(slot_total, BLK, BLK)
+    parts = (
+        gathered[:, slots_local * BLK :]
+        .reshape(total, VEC_ROWS * BLK)[:, : 3 * vec_local]
+        .reshape(total, 3, vec_local)
+        .astype(jnp.float32)
+    )
+    all_vector = ((parts[:, 2] + parts[:, 1]) + parts[:, 0]).reshape(-1)
+
     inverse = (
         jnp.zeros((slot_total,), jnp.int32)
         .at[owner_slot]
         .set(jnp.arange(slot_total, dtype=jnp.int32))
     )
-    matrices = split_matrices(all_slots[inverse[:NBLK]])
-    w_query, w_key, w_value, w_out, w_up, w_down = [
-        matrix.astype(jnp.bfloat16) for matrix in matrices
-    ]
+    w_query, w_key, w_value, w_out, w_up, w_down = split_matrices(all_slots[inverse[:NBLK]])
     b_query, b_value, b_out, gain_one, shift_one, b_up, b_down, gain_two, shift_two = split_vector(
         all_vector
     )
-    seq_local, tok_local, width = inputs.shape
     token_rows = inputs.reshape(seq_local * tok_local, width)
     local_shape = (seq_local, tok_local, width)
-    queries = (
-        (jnp.dot(token_rows, w_query, preferred_element_type=jnp.float32) + b_query)
-        .astype(jnp.bfloat16)
-        .reshape(local_shape)
-    )
-    keys_all = (
-        jnp.dot(token_rows, w_key, preferred_element_type=jnp.float32)
-        .astype(jnp.bfloat16)
-        .reshape(local_shape)
-    )
-    values_all = (
-        (jnp.dot(token_rows, w_value, preferred_element_type=jnp.float32) + b_value)
-        .astype(jnp.bfloat16)
-        .reshape(local_shape)
-    )
-    q_heads, k_heads, v_heads = (
-        lax.all_to_all(queries, "head", split_axis=2, concat_axis=1, tiled=True),
-        lax.all_to_all(keys_all, "head", split_axis=2, concat_axis=1, tiled=True),
-        lax.all_to_all(values_all, "head", split_axis=2, concat_axis=1, tiled=True),
-    )
-    length_full = q_heads.shape[1]
-    head_local = q_heads.shape[2] // HD
+    length_full = head_size * tok_local
+    full_rows = inputs_full.reshape(seq_local * length_full, width)
+    cols = width // head_size
+    begin = head_index * cols
+
+    def own(array):
+        return lax.dynamic_slice_in_dim(array, begin, cols, array.ndim - 1)
+
+    w_own = jnp.concatenate([own(w_query), own(w_key), own(w_value)], 1)
+    b_own = jnp.concatenate([own(b_query), jnp.zeros((cols,), jnp.float32), own(b_value)], 0)
+    qkv = (jnp.dot(full_rows, w_own, preferred_element_type=jnp.float32) + b_own).astype(
+        jnp.bfloat16
+    )
+    head_local = cols // HD
     scale = 1.0 / math.sqrt(HD)
     split_shape = (seq_local, length_full, head_local, HD)
-    q_split = q_heads.reshape(split_shape)
-    k_split = k_heads.reshape(split_shape)
-    v_split = v_heads.reshape(split_shape)
+    q_split = qkv[:, :cols].reshape(split_shape)
+    k_split = qkv[:, cols : 2 * cols].reshape(split_shape)
+    v_split = qkv[:, 2 * cols :].reshape(split_shape)
 
     def forward_item(items):
         return attend_forward(items[0], items[1], items[2], scale)
 
     context, log_total = lax.map(forward_item, (q_split, k_split, v_split))
-    context = context.reshape(seq_local, length_full, head_local * HD)
-    context_local = lax.all_to_all(
-        as_sent(context), "head", split_axis=1, concat_axis=2, tiled=True
-    ).astype(context.dtype)
-    context_rows = context_local.reshape(seq_local * tok_local, width)
+    context_rows = to_tokens(context.reshape(seq_local, length_full, cols), head_size, 2)
     branch = jnp.dot(context_rows, w_out, preferred_element_type=jnp.float32) + b_out
     z_one = token_rows.astype(jnp.float32) + branch
     first = layer_norm(z_one, gain_one, shift_one)
@@ -293,9 +767,9 @@
     d_branch = d_zone.astype(jnp.bfloat16)
     grad_out_w = weight_grad(context_rows, d_branch)
     grad_bout = jnp.sum(d_branch.astype(jnp.float32), axis=0)
-    d_context = back_product(d_branch, w_out).astype(jnp.bfloat16).reshape(local_shape)
-    d_context_heads = lax.all_to_all(d_context, "head", split_axis=2, concat_axis=1, tiled=True)
-    d_context_split = d_context_heads.reshape(split_shape)
+
+    d_context = back_product(d_branch, w_out).astype(jnp.bfloat16)
+    d_context_split = to_heads(d_context, seq_local, head_size, 3).reshape(split_shape)
 
     def backward_item(items):
         return attend_backward(items[0], items[1], items[2], items[3], items[4], scale)
@@ -303,42 +777,29 @@
     d_query, d_keys, d_values = lax.map(
         backward_item, (q_split, k_split, v_split, d_context_split, log_total)
     )
-    joined_shape = (seq_local, length_full, head_local * HD)
-    d_query_tok, d_keys_tok, d_values_tok = (
-        lax.all_to_all(
-            as_sent(d_query.reshape(joined_shape)), "head", split_axis=1, concat_axis=2, tiled=True
-        ),
-        lax.all_to_all(
-            as_sent(d_keys.reshape(joined_shape)), "head", split_axis=1, concat_axis=2, tiled=True
-        ),
-        lax.all_to_all(
-            as_sent(d_values.reshape(joined_shape)), "head", split_axis=1, concat_axis=2, tiled=True
-        ),
-    )
-    d_query_rows = d_query_tok.reshape(seq_local * tok_local, width)
-    d_keys_rows = d_keys_tok.reshape(seq_local * tok_local, width)
-    d_values_rows = d_values_tok.reshape(seq_local * tok_local, width)
-    grad_query = weight_grad(token_rows, d_query_rows)
-    grad_key = weight_grad(token_rows, d_keys_rows)
-    grad_value = weight_grad(token_rows, d_values_rows)
-    grad_bquery = jnp.sum(d_query_rows.astype(jnp.float32), axis=0)
-    grad_bvalue = jnp.sum(d_values_rows.astype(jnp.float32), axis=0)
-    input_grad = (
-        d_zone
-        + back_product(d_query_rows, w_query)
-        + back_product(d_keys_rows, w_key)
-        + back_product(d_values_rows, w_value)
-    )
-    input_grad = input_grad.reshape(local_shape)
-    grad_blocks = join_matrices([grad_query, grad_key, grad_value, grad_out_w, grad_up, grad_down])
-    padded = jnp.concatenate(
-        [grad_blocks, jnp.zeros((slot_total - grad_blocks.shape[0], BLK, BLK), jnp.float32)], 0
-    )
-    slot_terms = padded[owner_slot]
+    joined = (seq_local, length_full, cols)
+    d_all = jnp.concatenate(
+        [d_query.reshape(joined), d_keys.reshape(joined), d_values.reshape(joined)], 2
+    )
+    d_all_rows = d_all.reshape(seq_local * length_full, 3 * cols)
+    grad_own = weight_grad(full_rows, d_all_rows)
+    grad_b_own = jnp.sum(d_all_rows.astype(jnp.float32), axis=0)
+    d_local = to_tokens(d_all, head_size, 4, 3)
+    w_all = jnp.concatenate([w_query, w_key, w_value], 1)
+    input_grad = (d_zone + back_product(d_local, w_all)).reshape(local_shape)
+
+    def put(array):
+        empty = jnp.zeros(array.shape[:-1] + (width,), array.dtype)
+        return lax.dynamic_update_slice_in_dim(empty, array, begin, array.ndim - 1)
+
+    matrices = [put(grad_own[:, n * cols : (n + 1) * cols]) for n in range(3)]
+    blocks = join_matrices(
+        [matrix.astype(jnp.bfloat16) for matrix in matrices + [grad_out_w, grad_up, grad_down]]
+    )
     vector_terms = jnp.concatenate(
         [
-            grad_bquery,
-            grad_bvalue,
+            put(grad_b_own[:cols]),
+            put(grad_b_own[2 * cols :]),
             grad_bout,
             d_gain_one,
             d_shift_one,
@@ -348,11 +809,11 @@
             d_shift_two,
         ],
         0,
-    )
-    slot_grad, vec_grad = (
-        lax.psum_scatter(slot_terms, ("seq", "head"), scatter_dimension=0, tiled=True),
-        lax.psum_scatter(vector_terms, ("seq", "head"), scatter_dimension=0, tiled=True),
-    )
+    ).reshape(total, vec_local)
+    vec_terms = jnp.pad(vector_terms, ((0, 0), (0, VEC_ROWS * BLK - vec_local)))
+    vec_terms = vec_terms.astype(jnp.bfloat16).reshape(total, VEC_ROWS, BLK)
+    slot_grad, vec_sums = scatter_sums(dims, owner_slot, blocks, vec_terms)
+    vec_grad = vec_sums.reshape(-1)[:vec_local]
     first_moment, second_moment, updated = rotate_adam(
         slot_grad, master, moment_one, moment_two, basis_left, basis_right
     )

time: 645 us -> 464 us (0.72); the launches traced: 634 us -> 460 us
  waiting for transfers between devices: 215 us -> 0 us
  Pallas kernels: 0 us -> 211 us
  blocking collectives: 87.1 us -> 0 us
  starting transfers between devices: 36.8 us -> 0 us
  local copies, waits for them, and re-layouts: 155 us -> 135 us
  matrix products: 96.7 us -> 80 us
  between operations: 15.2 us -> 1.84 us
    pallas_call x0 -> x5, Pallas kernels: none -> 211 us  [the longest x1 82.2 us: scatter_sums(): pl.pallas_call(functools.partial(scatter_kernel, dims, slots), out_shape=...]
    reduce_scatter x1 -> x0, waiting for transfers between devices: 131 us -> none  [body(): lax.psum_scatter(slot_terms, ('seq', 'head'), scatter_dimension=0, tiled=...]
    unnamed x2 -> x0, blocking collectives: 87.1 us -> none
    all_to_all x8 -> x0, waiting for transfers between devices: 46.2 us -> none  [the longest x1 13.5 us: body(): lax.all_to_all(d_context, 'head', split_axis=2, concat_axis=1, tiled=True)]
    all_gather x1 -> x0, waiting for transfers between devices: 37.2 us -> none  [body(): lax.all_gather(master, ('seq', 'head'), axis=0, tiled=True)]
    all_to_all x8 -> x0, starting transfers between devices: 36.7 us -> none  [the longest x1 5.41 us: body(): lax.all_to_all(as_sent(context), 'head', split_axis=1, concat_axis=2, til...]
    transpose x0 -> x11, local copies, waits for them, and re-layouts: none -> 20.3 us  [the longest x6 9.61 us: build(): return pieces.reshape(row_count, col_count, BLK, BLK).transpose(0, 2, 1,...]
    reshape x9 -> x8, local copies, waits for them, and re-layouts: 29 us -> 10.3 us  [join_matrices(): matrix.reshape(row_count, BLK, col_count, BLK).transpose(0, 2, 1, 3)]
  transfers between devices with their start and end apart: 10 -> 0, of which waited for: 7 -> 0; matrix products, arithmetic and copies ran while one was open for 16% -> 0% of each run, Pallas kernels for 0% -> 0%
where the time goes in v1:
time: 464 us; the launch traced here: 460 us
  Pallas kernels  211 us (45%)
  local copies, waits for them, and re-layouts  135 us (29%)
  matrix products  80 us (17%)
  other arithmetic  31.3 us (7%)
    pallas_call x1, Pallas kernels, scatter_sums(): pl.pallas_call(functools.partial(scatter_kernel, dims, slots), out_shape=...  82.2 us
    pallas_call x1, Pallas kernels, gather_all(): pl.pallas_call(functools.partial(gather_kernel, dims), out_shape=(jax.Sha...  71.2 us
    pallas_call x3, Pallas kernels, exchange(): pl.pallas_call(functools.partial(exchange_kernel, head_size), out_shape=j...  57.6 us
    unnamed x124, local copies, waits for them, and re-layouts  23 us
    dot_general x4, matrix products, back_product(): jnp.einsum('to,io->ti', grads, weight, preferred_element_type=jnp.float32)  15.6 us
    gather x1, local copies, waits for them, and re-layouts, body(): all_slots[inverse[:NBLK]]  11.6 us
    concatenate x7, local copies, waits for them, and re-layouts, body(): jnp.concatenate([d_query.reshape(joined), d_keys.reshape(joined), d_value...  11.2 us
    reshape x8, local copies, waits for them, and re-layouts, join_matrices(): matrix.reshape(row_count, BLK, col_count, BLK).transpose(0, 2, 1, 3)  10.3 us

profile of v1, /device:TPU:11, one launch (start us, length us, event | category | flops | bytes accessed | tf_op | source)
XLA Modules:
  0.0 460.2 jit_solution(15648535645151018589)
XLA Ops:
  7.1 3.1 fusion.134
  10.2 71.2 %gather_all.1 = (bf16[3,4,256,512]{3,2,1,0:T(8,128)(2,1)}, bf16[32,1040,128]{2,1,0:T(8,128)(2,1)}) custom-call(bf16[3,256,512]{2,1,0:T(8,128)(2,1)} %x_ref.1, bf16[1040,128]{1,0:T(8,128)(2,1)} %pad_maximum_fusion.w_ref), custom_call_target="tpu_custom_call" | custom-call | tf_op jit(solution)/shard_map/gather_all/pallas_call | solution.py:383
  82.3 7.5 %slice.135 = bf16[32,1024,128]{2,1,0:T(8,128)(2,1)} slice(bf16[32,1040,128]{2,1,0:T(8,128)(2,1)} %get-tuple-element.99), slice={[0:32], [0:1024], [0:128]} | slice | bytes 16777216 | tf_op jit(solution)/shard_map/slice | solution.py:697
  89.8 11.6 %gather_fusion = bf16[192,128,128]{2,1,0:T(8,128)(2,1)} fusion(bf16[256,128,128]{2,1,0:T(8,128)(2,1)} %bitcast.362, s32[1024]{0:T(1024)S(1)} %pad_clamp_fusion), kind=kCustom, calls=%fused_computation | custom fusion | bytes 12583680 | tf_op jit(solution)/shard_map/gather | solution.py:711
  102.0 2.7 fusion.165
  104.7 4.0 fusion.164
  108.7 4.5 copy.74
  113.2 2.7 copy.73
  126.3 4.0 reshape.482
  130.3 3.5 copy.68
  135.5 3.5 copy.67
  139.9 20.3 %while.26 = (s32[]{:T(128)}, bf16[3,1024,2,64]{1,3,2,0:T(8,128)(2,1)}, f32[3,2,1024,1]{2,1,3,0:T(2,128)S(1)}, bf16[3,1024,2,64]{1,3,2,0:T(8,128)(2,1)S(1)}, bf16...) while((s32[]{:T(128)}, ...), condition=%wide.region_6.7_spmd, body=%wide.region_1.6_spmd.sunk | while | flops 556400640 | bytes 27347584 | solution.py:740
  160.3 2.9 reshape_reshape.6
  163.2 2.2 copy.70
  165.4 13.2 %exchange.3 = bf16[4,3,256,128]{3,2,1,0:T(8,128)(2,1)} custom-call(bf16[4,3,256,128]{3,2,1,0:T(8,128)(2,1)} %bitcast.375), custom_call_target="tpu_custom_call" | custom-call | tf_op jit(solution)/shard_map/exchange/pallas_call | solution.py:432
  182.4 2.5 multiply_convert_fusion.2
  192.0 4.9 %fusion.170 = (bf16[2048]{0:T(1024)(128)(2,1)S(1)}, bf16[768,2048]{1,0:T(8,128)(2,1)S(1)}) fusion(f32[768,2048]{1,0:T(8,128)S(1)} %get-tuple-element.243, f32[2048]{0:T(1024)S(1)} %slice.187, bf16[768,512]{1,0:T(8,128)(2,1)S(1)} %get-tuple-element.192, bf16[64,8,16,128]{3,2,1,0:T(8,128)(2,1)S(1)} %bitcast.383), kind=kOutput, calls=%fused_computation.263 | convolution fusion | flops 1629485056 | bytes 12333056 | tf_op jit(solution)/shard_map/to,io->ti/dot_general | solution.py:195
  196.9 3.2 convolution_convert_fusion
  200.1 3.4 multiply_reduce_fusion.4
  203.5 4.1 reshape.456
  207.6 3.7 copy.92
  219.1 2.8 convolution_convert_fusion.2
  224.7 13.2 %exchange.4 = bf16[4,3,256,128]{3,2,1,0:T(8,128)(2,1)} custom-call(bf16[4,3,256,128]{3,2,1,0:T(8,128)(2,1)} %bitcast.377), custom_call_target="tpu_custom_call" | custom-call | tf_op jit(solution)/shard_map/exchange/pallas_call | solution.py:432
  244.9 39.0 %while.27 = (s32[]{:T(128)}, bf16[3,1024,2,64]{1,3,2,0:T(8,128)(2,1)}, bf16[3,1024,2,64]{1,3,2,0:T(8,128)(2,1)}, bf16[3,1024,2,64]{1,3,2,0:T(8,128)(2,1)}, bf16[...) while((s32[]{:T(128)}, ...), condition=%wide.region_18.19_spmd, body=%wide.region_15.18_spmd.sunk | while | flops 1368782848 | bytes 72171200 | solution.py:777
  284.0 2.7 concatenate.80
  291.8 2.3 copy.80
  300.8 31.2 %exchange.5 = bf16[4,3,256,384]{3,2,1,0:T(8,128)(2,1)} custom-call(bf16[4,3,256,384]{3,2,1,0:T(8,128)(2,1)} %maximum_bitcast_fusion.1.src_ref), custom_call_target="tpu_custom_call" | custom-call | tf_op jit(solution)/shard_map/exchange/pallas_call | solution.py:432
  335.3 3.5 reshape.443
  338.8 5.8 %copy.83 = bf16[768,3,4,128]{0,3,2,1:T(8,128)(2,1)} copy(bf16[768,3,4,128]{3,1,0,2:T(4,128)(2,1)} %bitcast.363) | data formatting | bytes 4718592 | tf_op jit(solution)/shard_map/transpose | solution.py:651
  344.6 4.6 %add_add_fusion.3 = f32[768,512]{1,0:T(8,128)} fusion(f32[768,512]{1,0:T(8,128)S(1)} %copy-done.13, bf16[768,1536]{0,1:T(8,128)(2,1)} %bitcast.379, bf16[512,512]{1,0:T(8,128)(2,1)S(1)} %bitcast.400, bf16[512,512]{1,0:T(8,128)(2,1)} %bitcast.402, bf16[512,512]{1,0:T(8,128)(2,1)} %bitcast.404, f32[768]{0:T(1024)S(1)} %negate_multiply_fusion), kind=kOutput, calls=%fused_computation.152 | convolution fusion | flops 1213464576 | bytes 7080960 | tf_op jit(solution)/shard_map/to,io->ti/dot_general | solution.py:195
  369.5 82.2 %scatter_sums.1 = (f32[8,128,128]{2,1,0:T(8,128)}, f32[16,128]{1,0:T(8,128)}) custom-call(s32[256]{0:T(256)} %owner_ref.1, bf16[192,128,128]{2,1,0:T(8,128)(2,1)} %constant_dynamic-update-slice_fusion.3.blocks_ref, bf16[32,16,128]{2,1,0:T(8,128)(2,1)} %bitcast.409), custom_call_target="tpu_custom_call" | custom-call | tf_op jit(solution)/shard_map/scatter_sums/pallas_call | solution.py:611
  456.8 2.3 multiply_add_fusion.2
  (305 shorter events, 148.5 us)
Async XLA Ops:
  0.6 454.4 %copy-start = (f32[8,128,128]{2,1,0:T(8,128)S(1)}, f32[8,128,128]{2,1,0:T(8,128)}, u32[]{:S(2)}) copy-start(f32[8,128,128]{2,1,0:T(8,128)} %param.27) | copy-start | bytes 1572868
  113.2 2.7 copy-start.27
  113.2 3.9 copy-start.26
  118.5 2.7 copy-start.48
  126.3 7.5 %copy-start.18 = (bf16[3072,128]{1,0:T(8,128)(2,1)S(1)}, bf16[3072,128]{1,0:T(8,128)(2,1)}, u32[]{:S(2)}) copy-start(bf16[3072,128]{1,0:T(8,128)(2,1)} %get-tuple-element.221) | copy-start | bytes 2359300
  160.3 18.3 %copy-start.1 = (bf16[3,1024,2,64]{1,3,2,0:T(8,128)(2,1)}, bf16[3,1024,2,64]{1,3,2,0:T(8,128)(2,1)S(1)}, u32[]{:S(2)}) copy-start(bf16[3,1024,2,64]{1,3,2,0:T(8,128)(2,1)S(1)} %get-tuple-element.461) | copy-start | bytes 2359300
  163.2 16.8 %copy-start.35 = (bf16[4,128,4,128]{3,2,1,0:T(4,128)(2,1)S(1)}, bf16[4,128,4,128]{3,2,1,0:T(4,128)(2,1)}, u32[]{:S(2)}) copy-start(bf16[4,128,4,128]{3,2,1,0:T(4,128)(2,1)} %copy.72) | copy-start | bytes 1572868
  182.0 18.1 %copy-start.4 = (f32[768,512]{1,0:T(8,128)}, f32[768,512]{1,0:T(8,128)S(1)}, u32[]{:S(2)}) copy-start(f32[768,512]{1,0:T(8,128)S(1)} %get-tuple-element.241) | copy-start | bytes 4718596
  182.4 2.5 copy-start.23
  196.9 3.2 copy-start.19
  207.6 3.7 copy-start.5
  207.6 3.7 copy-start.28
  213.2 4.7 %copy-start.12 = (f32[768,512]{1,0:T(8,128)}, f32[768,512]{1,0:T(8,128)S(1)}, u32[]{:S(2)}) copy-start(f32[768,512]{1,0:T(8,128)S(1)} %get-tuple-element.196) | copy-start | bytes 4718596
  284.0 4.4 copy-start.9
  286.7 3.6 copy-start.11
  291.8 4.2 copy-start.10
  294.7 4.3 copy-start.17
  332.1 3.2 copy-start.6
  338.8 5.8 %copy-start.13 = (f32[768,512]{1,0:T(8,128)S(1)}, f32[768,512]{1,0:T(8,128)}, u32[]{:S(2)}) copy-start(f32[768,512]{1,0:T(8,128)} %copy-done.12) | copy-start | bytes 4718596
  338.8 5.8 %copy-start.30 = (bf16[64,8,4,128]{3,1,2,0:T(8,128)(2,1)S(1)}, bf16[64,8,4,128]{3,1,2,0:T(8,128)(2,1)}, u32[]{:S(2)}) copy-start(bf16[64,8,4,128]{3,1,2,0:T(8,128)(2,1)} %copy-done.29) | copy-start | bytes 1572868
  344.6 4.7 %copy-start.15 = (bf16[16,8,3,1024]{3,1,2,0:T(8,128)(2,1)S(1)}, bf16[16,8,3,1024]{3,1,2,0:T(8,128)(2,1)}, u32[]{:S(2)}) copy-start(bf16[16,8,3,1024]{3,1,2,0:T(8,128)(2,1)} %copy.114) | copy-start | bytes 2359300
  344.6 4.7 %copy-start.16 = (bf16[16,8,3,1024]{3,1,2,0:T(8,128)(2,1)S(1)}, bf16[16,8,3,1024]{3,1,2,0:T(8,128)(2,1)}, u32[]{:S(2)}) copy-start(bf16[16,8,3,1024]{3,1,2,0:T(8,128)(2,1)} %copy.115) | copy-start | bytes 2359300
  359.2 7.3 %copy-start.8 = (bf16[4,128,16,128]{3,1,2,0:T(8,128)(2,1)S(1)}, bf16[4,128,16,128]{3,1,2,0:T(8,128)(2,1)}, u32[]{:S(2)}) copy-start(bf16[4,128,16,128]{3,1,2,0:T(8,128)(2,1)} %copy.91) | copy-start | bytes 6291460
  369.5 82.3 %copy-start.45 = (f32[192]{0:T(256)S(1)}, f32[192]{0:T(256)}, u32[]{:S(2)}) copy-start(f32[192]{0:T(256)} %param.29) | copy-start | bytes 2308
  369.5 82.3 %copy-start.46 = (f32[192]{0:T(256)S(1)}, f32[192]{0:T(256)}, u32[]{:S(2)}) copy-start(f32[192]{0:T(256)} %param.31) | copy-start | bytes 2308
  369.5 82.3 %copy-start.47 = (f32[192]{0:T(256)S(1)}, f32[192]{0:T(256)}, u32[]{:S(2)}) copy-start(f32[192]{0:T(256)} %param.30) | copy-start | bytes 2308
  369.5 83.6 %copy-start.34 = (f32[8,128,128]{2,1,0:T(8,128)S(1)}, f32[8,128,128]{2,1,0:T(8,128)}, u32[]{:S(2)}) copy-start(f32[8,128,128]{2,1,0:T(8,128)} %param.26) | copy-start | bytes 1572868
  369.5 85.6 %copy-start.36 = (f32[8,128,128]{2,1,0:T(8,128)S(1)}, f32[8,128,128]{2,1,0:T(8,128)}, u32[]{:S(2)}) copy-start(f32[8,128,128]{2,1,0:T(8,128)} %param.25) | copy-start | bytes 1572868
  369.5 85.6 %copy-start.37 = (f32[8,128,128]{2,1,0:T(8,128)S(1)}, f32[8,128,128]{2,1,0:T(8,128)}, u32[]{:S(2)}) copy-start(f32[8,128,128]{2,1,0:T(8,128)} %param.24) | copy-start | bytes 1572868
  455.9 3.3 copy-start.39
  455.9 3.3 copy-start.40
  455.9 3.3 copy-start.21
  (20 other events, 32.7 us)

commit v2 on v1

--- a/solution.py
+++ b/solution.py
@@ -15,6 +15,8 @@
 STEP = 5
 HD = 64
 NBLK = 192
+QUERIES = 256
+SCALE = 1.0 / math.sqrt(HD)
 
 
 NORM_EPS = 1e-06
@@ -24,38 +26,6 @@
 DECAY = 0.01
 KEEP = 0.9
 HIGH = lax.Precision.HIGHEST
-
-
-def as_sent(array):
-
-    def short(part):
-        return part.astype(jnp.bfloat16) if part.dtype == jnp.float32 else part
-
-    return jax.tree.map(short, array)
-
-
-def split_matrices(blocks):
-    rows_d = D // BLK
-    cols_f = FF // BLK
-    square = rows_d * rows_d
-
-    def build(pieces, row_count, col_count):
-        return (
-            pieces.reshape(row_count, col_count, BLK, BLK)
-            .transpose(0, 2, 1, 3)
-            .reshape(row_count * BLK, col_count * BLK)
-        )
-
-    matrices = [
-        build(blocks[number * square : (number + 1) * square], rows_d, rows_d)
-        for number in range(4)
-    ]
-    offset = 4 * square
-    matrices.append(build(blocks[offset : offset + rows_d * cols_f], rows_d, cols_f))
-    matrices.append(
-        build(blocks[offset + rows_d * cols_f : offset + 2 * rows_d * cols_f], cols_f, rows_d)
-    )
-    return matrices
 
 
 def join_matrices(matrices):
@@ -105,73 +75,163 @@
     return ((within >= offsets) & (within < offsets + extents)).astype(jnp.float32)
 
 
-def attend_forward(query, keys_in, values_in, scale):
-    length_full = query.shape[0]
-    block = min(512, length_full)
-    outputs = []
-    totals = []
-    for begin_row in range(0, length_full, block):
-        scores = (
-            jnp.einsum(
-                "qhd,khd->hqk",
-                query[begin_row : begin_row + block],
-                keys_in,
-                preferred_element_type=jnp.float32,
-            )
-            * scale
-        )
-        highest = jnp.max(scores, axis=-1, keepdims=True)
-        weights_exp = jnp.exp(scores - highest)
-        summed = jnp.sum(weights_exp, axis=-1, keepdims=True)
-        probs = (weights_exp / summed).astype(jnp.bfloat16)
-        outputs.append(
-            jnp.einsum("hqk,khd->qhd", probs, values_in, preferred_element_type=jnp.float32)
-        )
-        totals.append(highest + jnp.log(summed))
-    return (jnp.concatenate(outputs, 0).astype(jnp.bfloat16), jnp.concatenate(totals, 1))
-
-
-def attend_backward(query, keys_in, values_in, grad_ctx, log_total, scale):
-    length_full = query.shape[0]
-    block = min(512, length_full)
-    grad_keys = jnp.zeros(keys_in.shape, jnp.float32)
-    grad_values = jnp.zeros(values_in.shape, jnp.float32)
-    grad_queries = []
-    for begin_row in range(0, length_full, block):
-        rows_query = query[begin_row : begin_row + block]
-        rows_grad = grad_ctx[begin_row : begin_row + block]
-        scores = (
-            jnp.einsum("qhd,khd->hqk", rows_query, keys_in, preferred_element_type=jnp.float32)
-            * scale
-        )
-        probs = jnp.exp(scores - log_total[:, begin_row : begin_row + block])
-        grad_probs = jnp.einsum(
-            "qhd,khd->hqk", rows_grad, values_in, preferred_element_type=jnp.float32
-        )
-        inner = jnp.sum(probs * grad_probs, axis=-1, keepdims=True)
-        grad_scores = (probs * (grad_probs - inner)).astype(jnp.bfloat16)
-        grad_queries.append(
-            jnp.einsum("hqk,khd->qhd", grad_scores, keys_in, preferred_element_type=jnp.float32)
-            * scale
-        )
-        grad_keys = (
-            grad_keys
-            + jnp.einsum(
-                "hqk,qhd->khd", grad_scores, rows_query, preferred_element_type=jnp.float32
-            )
-            * scale
-        )
-        grad_values = grad_values + jnp.einsum(
-            "hqk,qhd->khd",
-            probs.astype(jnp.bfloat16),
-            rows_grad,
-            preferred_element_type=jnp.float32,
-        )
-    return (
-        jnp.concatenate(grad_queries, 0).astype(jnp.bfloat16),
-        grad_keys.astype(jnp.bfloat16),
-        grad_values.astype(jnp.bfloat16),
-    )
+def contract(left, right, left_axis, right_axis):
+    return lax.dot_general(
+        left, right, (((left_axis,), (right_axis,)), ((), ())), preferred_element_type=jnp.float32
+    )
+
+
+def forward_kernel(x_ref, w_ref, b_ref, qkv_ref, ctx_ref, lse_ref):
+    head_size, tokens, width = x_ref.shape[0], x_ref.shape[1], x_ref.shape[2]
+    length = head_size * tokens
+    cols = w_ref.shape[1] // 3
+    rows = x_ref[...].reshape(length, width)
+    qkv_ref[...] = (contract(rows, w_ref[...], 1, 0) + b_ref[...]).astype(jnp.bfloat16)
+    step = min(QUERIES, tokens)
+    for number in range(cols // HD):
+        low = number * HD
+        keys = qkv_ref[:, cols + low : cols + low + HD]
+        values = qkv_ref[:, 2 * cols + low : 2 * cols + low + HD]
+        for begin in range(0, length, step):
+            query = qkv_ref[begin : begin + step, low : low + HD] * jnp.bfloat16(SCALE)
+            scores = contract(keys, query, 1, 1)
+            highest = jnp.max(scores, axis=0, keepdims=True)
+            weights = jnp.exp(scores - highest)
+            summed = jnp.sum(weights, axis=0, keepdims=True)
+            probs = (weights * (1.0 / summed)).astype(jnp.bfloat16)
+            context = contract(values, probs, 0, 0).T.astype(jnp.bfloat16)
+            ctx_ref[begin // tokens, pl.ds(begin % tokens, step), low : low + HD] = context
+            lse_ref[number : number + 1, begin : begin + step] = highest + jnp.log(summed)
+
+
+def attend(inputs_full, weights, bias):
+    seq_local, head_size, tokens, width = inputs_full.shape
+    length = head_size * tokens
+    cols = weights.shape[1] // 3
+    return pl.pallas_call(
+        forward_kernel,
+        grid=(seq_local,),
+        out_shape=(
+            jax.ShapeDtypeStruct((seq_local, length, 3 * cols), jnp.bfloat16),
+            jax.ShapeDtypeStruct((head_size, seq_local, tokens, cols), jnp.bfloat16),
+            jax.ShapeDtypeStruct((seq_local, 8, length), jnp.float32),
+        ),
+        in_specs=[
+            pl.BlockSpec((None, head_size, tokens, width), lambda s: (s, 0, 0, 0)),
+            pl.BlockSpec((width, 3 * cols), lambda s: (0, 0)),
+            pl.BlockSpec((1, 3 * cols), lambda s: (0, 0)),
+        ],
+        out_specs=(
+            pl.BlockSpec((None, length, 3 * cols), lambda s: (s, 0, 0)),
+            pl.BlockSpec((head_size, None, tokens, cols), lambda s: (0, s, 0, 0)),
+            pl.BlockSpec((None, 8, length), lambda s: (s, 0, 0)),
+        ),
+        compiler_params=pltpu.CompilerParams(vmem_limit_bytes=48 * 1024 * 1024),
+        name="attend",
+    )(inputs_full, weights, bias)
+
+
+def backward_kernel(x_ref, qkv_ref, lse_ref, dctx_ref, grad_ref, dw_ref, db_ref, dall, acc):
+    head_size, tokens, width = x_ref.shape[0], x_ref.shape[1], x_ref.shape[2]
+    length = head_size * tokens
+    cols = qkv_ref.shape[1] // 3
+    step = min(QUERIES, tokens)
+    scale = jnp.bfloat16(SCALE)
+    for number in range(cols // HD):
+        low = number * HD
+        keys = qkv_ref[:, cols + low : cols + low + HD]
+        values = qkv_ref[:, 2 * cols + low : 2 * cols + low + HD]
+        for begin in range(0, length, step):
+            query = qkv_ref[begin : begin + step, low : low + HD] * scale
+            dctx = dctx_ref[begin // tokens, pl.ds(begin % tokens, step), low : low + HD]
+            scores = contract(keys, query, 1, 1)
+            probs = jnp.exp(scores - lse_ref[number : number + 1, begin : begin + step])
+            dprobs = contract(values, dctx, 1, 1)
+            inner = jnp.sum(probs * dprobs, axis=0, keepdims=True)
+            dscores = (probs * (dprobs - inner)).astype(jnp.bfloat16)
+            dkey = contract(dscores, query, 1, 0)
+            dvalue = contract(probs.astype(jnp.bfloat16), dctx, 1, 0)
+            if begin == 0:
+                acc[0] = dkey
+                acc[1] = dvalue
+            else:
+                acc[0] += dkey
+                acc[1] += dvalue
+            dquery = contract(keys, dscores, 0, 0).T * SCALE
+            dall[begin : begin + step, low : low + HD] = dquery.astype(jnp.bfloat16)
+        dall[:, cols + low : cols + low + HD] = acc[0].astype(jnp.bfloat16)
+        dall[:, 2 * cols + low : 2 * cols + low + HD] = acc[1].astype(jnp.bfloat16)
+    rows = x_ref[...].reshape(length, width)
+    delta = dall[...]
+    grad_ref[...] = delta.reshape(head_size, tokens, 3 * cols)
+    dw = contract(rows, delta, 0, 0)
+    db = jnp.sum(delta.astype(jnp.float32), axis=0, keepdims=True)
+
+    @pl.when(pl.program_id(0) == 0)
+    def _():
+        dw_ref[...] = dw
+        db_ref[...] = db
+
+    @pl.when(pl.program_id(0) > 0)
+    def _():
+        dw_ref[...] += dw
+        db_ref[...] += db
+
+
+def attend_back(inputs_full, qkv, lse, dctx):
+    seq_local, head_size, tokens, width = inputs_full.shape
+    length = head_size * tokens
+    cols = qkv.shape[2] // 3
+    return pl.pallas_call(
+        backward_kernel,
+        grid=(seq_local,),
+        out_shape=(
+            jax.ShapeDtypeStruct((head_size, seq_local, tokens, 3 * cols), jnp.bfloat16),
+            jax.ShapeDtypeStruct((width, 3 * cols), jnp.float32),
+            jax.ShapeDtypeStruct((1, 3 * cols), jnp.float32),
+        ),
+        in_specs=[
+            pl.BlockSpec((None, head_size, tokens, width), lambda s: (s, 0, 0, 0)),
+            pl.BlockSpec((None, length, 3 * cols), lambda s: (s, 0, 0)),
+            pl.BlockSpec((None, 8, length), lambda s: (s, 0, 0)),
+            pl.BlockSpec((head_size, None, tokens, cols), lambda s: (0, s, 0, 0)),
+        ],
+        out_specs=(
+            pl.BlockSpec((head_size, None, tokens, 3 * cols), lambda s: (0, s, 0, 0)),
+            pl.BlockSpec((width, 3 * cols), lambda s: (0, 0)),
+            pl.BlockSpec((1, 3 * cols), lambda s: (0, 0)),
+        ),
+        scratch_shapes=[
+            pltpu.VMEM((length, 3 * cols), jnp.bfloat16),
+            pltpu.VMEM((2, length, HD), jnp.float32),
+        ],
+        compiler_params=pltpu.CompilerParams(vmem_limit_bytes=48 * 1024 * 1024),
+        name="attend_back",
+    )(inputs_full, qkv, lse, dctx)
+
+
+def input_grad_kernel(dz_ref, d_ref, w_ref, out_ref):
+    total = dz_ref[...]
+    for number in range(d_ref.shape[0]):
+        total = total + contract(d_ref[number], w_ref[number], 1, 1)
+    out_ref[...] = total
+
+
+def input_grads(d_zone, deltas, weights):
+    head_size, seq_local, tokens, columns = deltas.shape
+    width = d_zone.shape[1]
+    return pl.pallas_call(
+        input_grad_kernel,
+        grid=(seq_local,),
+        out_shape=jax.ShapeDtypeStruct((seq_local, tokens, width), jnp.float32),
+        in_specs=[
+            pl.BlockSpec((tokens, width), lambda s: (s, 0)),
+            pl.BlockSpec((head_size, None, tokens, columns), lambda s: (0, s, 0, 0)),
+            pl.BlockSpec((head_size, width, columns), lambda s: (0, 0, 0)),
+        ],
+        out_specs=pl.BlockSpec((None, tokens, width), lambda s: (s, 0, 0)),
+        name="input_grads",
+    )(d_zone, deltas, weights)
 
 
 def rotate_adam(grads, master, moment_one, moment_two, basis_left, basis_right):
@@ -197,6 +257,7 @@
 
 MESH = pl.DeviceIdType.MESH
 VEC_ROWS = 16
+PIECE = 16
 
 
 def cut(seq_size, head_size):
@@ -260,13 +321,33 @@
 
 
 def gather_kernel(
-    dims, x_ref, w_ref, xf_ref, wf_ref, own_sem, x_send, x_recv, w_send, w_recv
+    dims,
+    inv_ref,
+    x_ref,
+    w_ref,
+    xf_ref,
+    qkv_ref,
+    out_ref,
+    up_ref,
+    down_ref,
+    vec_ref,
+    wf_ref,
+    own_sem,
+    x_send,
+    x_recv,
+    w_send,
+    w_recv,
 ):
     me = place(dims)
     size_z, size_x, size_y, size_c = dims
     head_me = me[2] * size_c + me[3]
+    chunk = w_ref.shape[0]
+
+    def spot(index):
+        return wf_ref.at[pl.ds(index * chunk, chunk)]
+
     own_x = pltpu.make_async_copy(x_ref, xf_ref.at[:, head_me], own_sem.at[0])
-    own_w = pltpu.make_async_copy(w_ref, wf_ref.at[flat(dims, me)], own_sem.at[1])
+    own_w = pltpu.make_async_copy(w_ref, spot(flat(dims, me)), own_sem.at[1])
     own_x.start()
     own_w.start()
     greet(dims, me)
@@ -301,7 +382,7 @@
         count[0] = number + 1
         copy = pltpu.make_async_remote_copy(
             src_ref=source,
-            dst_ref=wf_ref.at[index],
+            dst_ref=spot(index),
             send_sem=w_send.at[number],
             recv_sem=w_recv.at[index],
             device_id=device(dims, target),
@@ -313,7 +394,7 @@
     def arrived_w(index):
         pltpu.make_async_remote_copy(
             src_ref=w_ref,
-            dst_ref=wf_ref.at[index],
+            dst_ref=spot(index),
             send_sem=w_send.at[0],
             recv_sem=w_recv.at[index],
             device_id=device(dims, me),
@@ -343,7 +424,7 @@
             for coords in held:
                 source = moved(dims, coords, axis, step)
                 arrived_w(flat(dims, source))
-                forward(wf_ref.at[flat(dims, source)], source, level + 1)
+                forward(spot(flat(dims, source)), source, level + 1)
                 fresh.append(source)
         held = held + fresh
         if level == 1:
@@ -364,9 +445,59 @@
         copy.wait_send()
     own_x.wait()
     own_w.wait()
-
-
-def gather_all(dims, inputs, packed):
+    unpack(dims, inv_ref, wf_ref, qkv_ref, out_ref, up_ref, down_ref)
+    chunk = w_ref.shape[0]
+    for number in range(vec_ref.shape[0]):
+        vec_ref[number] = wf_ref[(number + 1) * chunk - 1]
+
+
+def unpack(dims, inv_ref, wf_ref, qkv_ref, out_ref, up_ref, down_ref):
+    head_size = dims[2] * dims[3]
+    width = out_ref.shape[0]
+    hidden = up_ref.shape[1]
+    cols = width // head_size
+    across = width // BLK
+
+    def block(number):
+        piece = inv_ref[number]
+        return jnp.concatenate([wf_ref[piece + part] for part in range(BLK // PIECE)], 0)
+
+    def rows_of(row_count, first, col_count, store):
+        def one(row, carry):
+            span = pl.ds(pl.multiple_of(row * BLK, BLK), BLK)
+            for col in range(col_count):
+                store(span, col, block(first + row * col_count + col))
+            return carry
+
+        lax.fori_loop(0, row_count, one, 0)
+
+    for number in range(3):
+
+        def store_qkv(span, col, value, number=number):
+            for begin in range(0, BLK, min(cols, BLK)):
+                head = (col * BLK + begin) // cols
+                lane = (col * BLK + begin) % cols
+                part = min(cols, BLK)
+                qkv_ref[head, span, number * cols + lane : number * cols + lane + part] = value[
+                    :, begin : begin + part
+                ]
+
+        rows_of(across, number * across * across, across, store_qkv)
+
+    def store_in(ref):
+        def store(span, col, value):
+            ref[span, col * BLK : (col + 1) * BLK] = value
+
+        return store
+
+    rows_of(across, 3 * across * across, across, store_in(out_ref))
+    first = 4 * across * across
+    rows_of(across, first, hidden // BLK, store_in(up_ref))
+    first = first + across * (hidden // BLK)
+    rows_of(hidden // BLK, first, across, store_in(down_ref))
+
+
+def gather_all(dims, inverse, inputs, packed):
     size_z, size_x, size_y, size_c = dims
     total = size_z * size_x * size_y * size_c
     head_size = size_y * size_c
@@ -384,20 +515,27 @@
         functools.partial(gather_kernel, dims),
         out_shape=(
             jax.ShapeDtypeStruct((seq_local, head_size, tok_local, width), inputs.dtype),
-            jax.ShapeDtypeStruct((total,) + packed.shape, packed.dtype),
+            jax.ShapeDtypeStruct((head_size, width, 3 * width // head_size), packed.dtype),
+            jax.ShapeDtypeStruct((width, width), packed.dtype),
+            jax.ShapeDtypeStruct((width, FF), packed.dtype),
+            jax.ShapeDtypeStruct((FF, width), packed.dtype),
+            jax.ShapeDtypeStruct((total, VEC_ROWS, BLK), packed.dtype),
         ),
-        in_specs=[whole, whole],
-        out_specs=(any_space, any_space),
+        in_specs=[pl.BlockSpec(memory_space=pltpu.SMEM), whole, whole],
+        out_specs=(any_space, whole, whole, whole, whole, whole),
         scratch_shapes=[
+            pltpu.VMEM((total * packed.shape[0],) + packed.shape[1:], packed.dtype),
             pltpu.SemaphoreType.DMA((2,)),
             pltpu.SemaphoreType.DMA((max(sends_x, 1),)),
             pltpu.SemaphoreType.DMA((head_size,)),
             pltpu.SemaphoreType.DMA((max(sends_w, 1),)),
             pltpu.SemaphoreType.DMA((total,)),
         ],
-        compiler_params=pltpu.CompilerParams(collective_id=0, has_side_effects=True),
+        compiler_params=pltpu.CompilerParams(
+            collective_id=0, has_side_effects=True, vmem_limit_bytes=40 * 1024 * 1024
+        ),
         name="gather_all",
-    )(inputs, packed)
+    )(inverse, inputs, packed)
 
 
 def exchange_kernel(head_size, src_ref, dst_ref, own_sem, send_sem, recv_sem):
@@ -643,21 +781,6 @@
     return -(-value // unit) * unit
 
 
-def to_tokens(array, head_size, number, parts=1):
-    seq_local, length, columns = array.shape
-    tokens = length // head_size
-    array = array.reshape(seq_local, head_size, tokens, columns).transpose(1, 0, 2, 3)
-    got = exchange(array, number).reshape(head_size, seq_local * tokens, parts, columns // parts)
-    return got.transpose(1, 2, 0, 3).reshape(seq_local * tokens, head_size * columns)
-
-
-def to_heads(rows, seq_local, head_size, number):
-    columns = rows.shape[1] // head_size
-    array = rows.reshape(seq_local, rows.shape[0] // seq_local, head_size, columns)
-    got = exchange(array.transpose(2, 0, 1, 3), number)
-    return got.transpose(1, 0, 2, 3).reshape(seq_local, -1, columns)
-
-
 def body(
     inputs,
     cotangent,
@@ -692,53 +815,39 @@
             as_rows(jnp.concatenate(three_parts(vec_master)), VEC_ROWS),
         ],
         0,
-    )
-    inputs_full, gathered = gather_all(dims, inputs, packed)
-    all_slots = gathered[:, : slots_local * BLK].reshape(slot_total, BLK, BLK)
+    ).reshape(-1, PIECE, BLK)
+    numbers = jnp.arange(slot_total, dtype=jnp.int32)
+    inverse = jnp.sum(
+        jnp.where(owner_slot[:, None] == numbers[None, :], numbers[:, None], 0), axis=0
+    )
+    pieces = (inverse // slots_local) * packed.shape[0]
+    pieces = pieces + (inverse % slots_local) * (BLK // PIECE)
+    inputs_full, w_qkv, w_out, w_up, w_down, vec_parts = gather_all(
+        dims, pieces, inputs, packed
+    )
     parts = (
-        gathered[:, slots_local * BLK :]
+        vec_parts
         .reshape(total, VEC_ROWS * BLK)[:, : 3 * vec_local]
         .reshape(total, 3, vec_local)
         .astype(jnp.float32)
     )
     all_vector = ((parts[:, 2] + parts[:, 1]) + parts[:, 0]).reshape(-1)
 
-    inverse = (
-        jnp.zeros((slot_total,), jnp.int32)
-        .at[owner_slot]
-        .set(jnp.arange(slot_total, dtype=jnp.int32))
-    )
-    w_query, w_key, w_value, w_out, w_up, w_down = split_matrices(all_slots[inverse[:NBLK]])
     b_query, b_value, b_out, gain_one, shift_one, b_up, b_down, gain_two, shift_two = split_vector(
         all_vector
     )
     token_rows = inputs.reshape(seq_local * tok_local, width)
     local_shape = (seq_local, tok_local, width)
-    length_full = head_size * tok_local
-    full_rows = inputs_full.reshape(seq_local * length_full, width)
     cols = width // head_size
     begin = head_index * cols
 
     def own(array):
         return lax.dynamic_slice_in_dim(array, begin, cols, array.ndim - 1)
 
-    w_own = jnp.concatenate([own(w_query), own(w_key), own(w_value)], 1)
+    w_own = lax.dynamic_index_in_dim(w_qkv, head_index, 0, keepdims=False)
     b_own = jnp.concatenate([own(b_query), jnp.zeros((cols,), jnp.float32), own(b_value)], 0)
-    qkv = (jnp.dot(full_rows, w_own, preferred_element_type=jnp.float32) + b_own).astype(
-        jnp.bfloat16
-    )
-    head_local = cols // HD
-    scale = 1.0 / math.sqrt(HD)
-    split_shape = (seq_local, length_full, head_local, HD)
-    q_split = qkv[:, :cols].reshape(split_shape)
-    k_split = qkv[:, cols : 2 * cols].reshape(split_shape)
-    v_split = qkv[:, 2 * cols :].reshape(split_shape)
-
-    def forward_item(items):
-        return attend_forward(items[0], items[1], items[2], scale)
-
-    context, log_total = lax.map(forward_item, (q_split, k_split, v_split))
-    context_rows = to_tokens(context.reshape(seq_local, length_full, cols), head_size, 2)
+    qkv, context, log_total = attend(inputs_full, w_own, b_own[None, :])
+    context_rows = exchange(context, 2).transpose(1, 2, 0, 3).reshape(seq_local * tok_local, width)
     branch = jnp.dot(context_rows, w_out, preferred_element_type=jnp.float32) + b_out
     z_one = token_rows.astype(jnp.float32) + branch
     first = layer_norm(z_one, gain_one, shift_one)
@@ -769,24 +878,12 @@
     grad_bout = jnp.sum(d_branch.astype(jnp.float32), axis=0)
 
     d_context = back_product(d_branch, w_out).astype(jnp.bfloat16)
-    d_context_split = to_heads(d_context, seq_local, head_size, 3).reshape(split_shape)
-
-    def backward_item(items):
-        return attend_backward(items[0], items[1], items[2], items[3], items[4], scale)
-
-    d_query, d_keys, d_values = lax.map(
-        backward_item, (q_split, k_split, v_split, d_context_split, log_total)
-    )
-    joined = (seq_local, length_full, cols)
-    d_all = jnp.concatenate(
-        [d_query.reshape(joined), d_keys.reshape(joined), d_values.reshape(joined)], 2
-    )
-    d_all_rows = d_all.reshape(seq_local * length_full, 3 * cols)
-    grad_own = weight_grad(full_rows, d_all_rows)
-    grad_b_own = jnp.sum(d_all_rows.astype(jnp.float32), axis=0)
-    d_local = to_tokens(d_all, head_size, 4, 3)
-    w_all = jnp.concatenate([w_query, w_key, w_value], 1)
-    input_grad = (d_zone + back_product(d_local, w_all)).reshape(local_shape)
+    d_context = d_context.reshape(seq_local, tok_local, head_size, cols).transpose(2, 0, 1, 3)
+    d_all, grad_own, grad_b_own = attend_back(
+        inputs_full, qkv, log_total, exchange(d_context, 3)
+    )
+    grad_b_own = grad_b_own.reshape(-1)
+    input_grad = input_grads(d_zone, exchange(d_all, 4), w_qkv)
 
     def put(array):
         empty = jnp.zeros(array.shape[:-1] + (width,), array.dtype)

time: 464 us -> 352 us (0.76)
  local copies, waits for them, and re-layouts: 135 us -> 38.7 us
  Pallas kernels: 211 us -> 269 us
  matrix products: 80 us -> 27.5 us
  other arithmetic: 31.3 us -> 8.97 us
    pallas_call x0 -> x3, Pallas kernels: none -> 56.8 us  [the longest x1 27.8 us: attend_back(): pl.pallas_call(backward_kernel, grid=(seq_local,), out_shape=(jax.ShapeDt...]
    dot_general x43 -> x0, matrix products: 44.1 us -> none  [the longest x6 8.6 us: attend_backward(): jnp.einsum('qhd,khd->hqk', rows_grad, values_in, preferred_element_type=j...]
    slice x5 -> x0, local copies, waits for them, and re-layouts: 16.8 us -> none  [the longest x1 7.53 us: body(): all_slots = gathered[:, :slots_local * BLK].reshape(slot_total, BLK, BLK)]
    transpose x8 -> x1, local copies, waits for them, and re-layouts: 17.7 us -> 1.74 us  [body(): exchange(context, 2).transpose(1, 2, 0, 3)]
    gather x1 -> x0, local copies, waits for them, and re-layouts: 11.6 us -> none  [body(): all_slots[inverse[:NBLK]]]
    while x12 -> x0, local copies, waits for them, and re-layouts: 11.4 us -> none  [the longest x3 8.11 us: body(): context, log_total = lax.map(forward_item, (q_split, k_split, v_split))]
    reshape x7 -> x2, local copies, waits for them, and re-layouts: 14 us -> 2.77 us  [body(): d_context.reshape(seq_local, tok_local, head_size, cols)]
    concatenate x7 -> x0, local copies, waits for them, and re-layouts: 11.2 us -> none  [body(): jnp.concatenate([d_query.reshape(joined), d_keys.reshape(joined), d_value...]
where the time goes in v2:
time: 352 us; the launch traced here: 346 us
  Pallas kernels  269 us (76%)
  local copies, waits for them, and re-layouts  38.7 us (11%)
  matrix products  27.5 us (8%)
  other arithmetic  8.97 us (3%)
    pallas_call x1, Pallas kernels, scatter_sums(): pl.pallas_call(functools.partial(scatter_kernel, dims, slots), out_shape=...  82.1 us
    pallas_call x1, Pallas kernels, gather_all(): pl.pallas_call(functools.partial(gather_kernel, dims), out_shape=(jax.Sha...  71.6 us
    pallas_call x3, Pallas kernels, exchange(): pl.pallas_call(functools.partial(exchange_kernel, head_size), out_shape=j...  58.2 us
    pallas_call x1, Pallas kernels, attend_back(): pl.pallas_call(backward_kernel, grid=(seq_local,), out_shape=(jax.ShapeDt...  27.8 us
    unnamed x96, local copies, waits for them, and re-layouts  23.6 us
    pallas_call x1, Pallas kernels, attend(): pl.pallas_call(forward_kernel, grid=(seq_local,), out_shape=(jax.ShapeDty...  23.3 us
    dot_general x3, matrix products, back_product(): jnp.einsum('to,io->ti', grads, weight, preferred_element_type=jnp.float32)  8.66 us
    dot_general x3, matrix products, weight_grad(): jnp.einsum('ti,to->io', left, right, preferred_element_type=jnp.float32)  7.78 us

profile of v2, /device:TPU:11, one launch (start us, length us, event | category | flops | bytes accessed | tf_op | source)
XLA Modules:
  0.0 345.5 jit_solution(5405966100448047869)
XLA Ops:
  3.3 2.6 fusion.22
  6.0 71.6 %gather_all.1 = (bf16[3,4,256,512]{3,2,1,0:T(8,128)(2,1)S(1)}, bf16[4,512,384]{2,1,0:T(8,128)(2,1)S(1)}, bf16[512,512]{1,0:T(8,128)(2,1)S(1)}, bf16[512,2048]{1,...) custom-call(s32[256]{0:T(256)S(1)} %get-tuple-element.86.inv_ref, ...), custom_call_target="tpu_custom_call" | custom-call | tf_op jit(solution)/shard_map/gather_all/pallas_call | solution.py:514
  77.6 1.6 copy-done.1
  80.0 1.3 copy-done.10
  81.4 1.3 copy-done.12
  83.3 23.3 %attend.1 = (bf16[3,1024,384]{2,1,0:T(8,128)(2,1)S(1)}, bf16[4,3,256,128]{3,2,1,0:T(8,128)(2,1)S(1)}, f32[3,8,1024]{2,1,0:T(8,128)S(1)}) custom-call(bf16[3,4,256,512]{3,2,1,0:T(8,128)(2,1)} %copy-done.1, bf16[512,384]{1,0:T(8,128)(2,1)S(1)} %dynamic-slice_bitcast_fusion.w_ref, f32[1,384]{1,0:T(1,128)S(1)} %broadcast_in_dim.31.b_ref), custom_call_target="tpu_custom_call" | custom-call | tf_op jit(solution)/shard_map/attend/pallas_call | solution.py:111
  106.6 1.5 copy-done.4
  109.0 13.8 %exchange.3 = bf16[4,3,256,128]{3,2,1,0:T(8,128)(2,1)} custom-call(bf16[4,3,256,128]{3,2,1,0:T(8,128)(2,1)} %copy-done.7), custom_call_target="tpu_custom_call" | custom-call | tf_op jit(solution)/shard_map/exchange/pallas_call | solution.py:570
  122.8 1.7 copy.37
  126.5 2.3 multiply_convert_fusion
  128.8 2.1 fusion.54
  132.9 1.6 fusion.51
  134.7 4.4 %fusion.55 = (bf16[2048]{0:T(1024)(128)(2,1)S(1)}, bf16[768,2048]{1,0:T(8,128)(2,1)S(1)}) fusion(f32[768,2048]{1,0:T(8,128)S(1)} %get-tuple-element.78, f32[2048]{0:T(1024)S(1)} %slice.93, bf16[768,512]{1,0:T(8,128)(2,1)S(1)} %get-tuple-element.50, bf16[2048,512]{1,0:T(8,128)(2,1)S(1)} %copy-done.13), kind=kOutput, calls=%fused_computation.126 | convolution fusion | flops 1629485056 | bytes 12333056 | tf_op jit(solution)/shard_map/to,io->ti/dot_general | solution.py:255
  139.1 2.8 multiply_reduce_fusion
  142.8 1.5 convolution_convert_fusion.2
  144.3 1.7 reshape.241
  147.1 13.4 %exchange.4.dctx_ref = bf16[4,3,256,128]{3,2,1,0:T(8,128)(2,1)} custom-call(bf16[4,3,256,128]{3,2,1,0:T(8,128)(2,1)} %bitcast.89), custom_call_target="tpu_custom_call" | custom-call | tf_op jit(solution)/shard_map/exchange/pallas_call | solution.py:570
  161.6 27.8 %attend_back.1 = (bf16[4,3,256,384]{3,2,1,0:T(8,128)(2,1)S(1)}, f32[512,384]{1,0:T(8,128)S(1)}, f32[1,384]{1,0:T(1,128)S(1)}) custom-call(bf16[3,4,256,512]{3,2,1,0:T(8,128)(2,1)} %copy-done.1, bf16[3,1024,384]{2,1,0:T(8,128)(2,1)} %copy-done.4, f32[3,8,1024]{2,1,0:T(8,128)S(1)} %get-tuple-element.34.lse_ref, bf16[4,3,256,128]{3,2,1,0:T(8,128)(2,1)S(1)} %copy-done.2), custom_call_target="tpu_custom_call" | custom-call | tf_op jit(solution)/shard_map/attend_back/pallas_call | solution.py:185
  189.4 1.4 copy-done.5
  190.8 31.0 %exchange.5.d_ref = bf16[4,3,256,384]{3,2,1,0:T(8,128)(2,1)} custom-call(bf16[4,3,256,384]{3,2,1,0:T(8,128)(2,1)} %copy-done.5), custom_call_target="tpu_custom_call" | custom-call | tf_op jit(solution)/shard_map/exchange/pallas_call | solution.py:570
  221.8 5.8 %input_grads.1 = f32[3,256,512]{2,1,0:T(8,128)} custom-call(f32[768,512]{1,0:T(8,128)} %copy-done.14, bf16[4,3,256,384]{3,2,1,0:T(8,128)(2,1)} %exchange.5.d_ref, bf16[4,512,384]{2,1,0:T(8,128)(2,1)} %copy-done.3), custom_call_target="tpu_custom_call" | custom-call | tf_op jit(solution)/shard_map/input_grads/pallas_call | solution.py:223
  230.9 1.1 copy.41
  235.1 4.0 %fusion.6 = bf16[64,8,16,128]{3,1,2,0:T(8,128)(2,1)S(1)} fusion(bf16[768,2048]{1,0:T(8,128)(2,1)} %copy-done.21, f32[768,512]{1,0:T(8,128)S(1)} %copy-done.18, f32[512]{0:T(512)S(1)} %get-tuple-element.67, f32[512]{0:T(512)S(1)} %get-tuple-element.68, f32[768]{0:T(1024)S(1)} %fusion.34, f32[768]{0:T(1024)S(1)} %broadcast_multiply_fusion.1), kind=kOutput, calls=%fused_computation.13 | convolution fusion | flops 1613627392 | bytes 6825984 | tf_op jit(solution)/shard_map/ti,to->io/dot_general | solution.py:251
  240.3 1.5 constant_dynamic-update-slice_fusion.1
  241.7 1.4 copy-done.38
  243.2 3.2 convolution_convert_fusion
  246.4 2.5 reshape.252
  249.5 1.5 constant_dynamic-update-slice_fusion.blocks_ref
  254.2 82.1 %scatter_sums.1 = (f32[8,128,128]{2,1,0:T(8,128)}, f32[16,128]{1,0:T(8,128)}) custom-call(s32[256]{0:T(256)} %owner_ref.1, bf16[192,128,128]{2,1,0:T(8,128)(2,1)} %constant_dynamic-update-slice_fusion.blocks_ref, bf16[32,16,128]{2,1,0:T(8,128)(2,1)} %bitcast.101), custom_call_target="tpu_custom_call" | custom-call | tf_op jit(solution)/shard_map/scatter_sums/pallas_call | solution.py:749
  336.3 1.4 divide_subtract_fusion
  337.7 2.0 fusion.56
  342.1 2.3 multiply_add_fusion.2
  (155 shorter events, 26.5 us)
Async XLA Ops:
  0.6 339.1 %copy-start = (f32[8,128,128]{2,1,0:T(8,128)S(1)}, f32[8,128,128]{2,1,0:T(8,128)}, u32[]{:S(2)}) copy-start(f32[8,128,128]{2,1,0:T(8,128)} %param.23) | copy-start | bytes 1572868
  0.7 5.2 %copy-start.33 = (f32[192]{0:T(256)S(1)}, f32[192]{0:T(256)}, u32[]{:S(2)}) copy-start(f32[192]{0:T(256)} %param.25) | copy-start | bytes 2308
  0.7 5.3 %copy-start.23 = (f32[8,128,128]{2,1,0:T(8,128)S(1)}, f32[8,128,128]{2,1,0:T(8,128)}, u32[]{:S(2)}) copy-start(f32[8,128,128]{2,1,0:T(8,128)} %param.19) | copy-start | bytes 1572868
  3.3 2.8 copy-start.6
  77.6 1.6 copy-start.1
  82.7 23.9 %copy-start.3 = (bf16[4,512,384]{2,1,0:T(8,128)(2,1)}, bf16[4,512,384]{2,1,0:T(8,128)(2,1)S(1)}, u32[]{:S(2)}) copy-start(bf16[4,512,384]{2,1,0:T(8,128)(2,1)S(1)} %get-tuple-element.27.w_ref) | copy-start | bytes 4718596
  106.6 1.5 copy-start.4
  109.0 15.6 %copy-start.9 = (bf16[512,512]{1,0:T(8,128)(2,1)S(1)}, bf16[512,512]{1,0:T(8,128)(2,1)}, u32[]{:S(2)}) copy-start(bf16[512,512]{1,0:T(8,128)(2,1)} %copy-done.8) | copy-start | bytes 1572868
  124.5 1.9 copy-start.11
  125.4 16.5 %copy-start.17 = (f32[768,512]{1,0:T(8,128)}, f32[768,512]{1,0:T(8,128)S(1)}, u32[]{:S(2)}) copy-start(f32[768,512]{1,0:T(8,128)S(1)} %get-tuple-element.76) | copy-start | bytes 4718596
  126.5 2.3 copy-start.13
  128.8 2.1 copy-start.37
  134.7 4.4 %copy-start.25 = (bf16[768,512]{1,0:T(8,128)(2,1)}, bf16[768,512]{1,0:T(8,128)(2,1)S(1)}, u32[]{:S(2)}) copy-start(bf16[768,512]{1,0:T(8,128)(2,1)S(1)} %get-tuple-element.50) | copy-start | bytes 2359300
  139.1 2.8 copy-start.21
  142.8 3.3 copy-start.14
  189.4 1.4 copy-start.5
  230.0 2.9 copy-start.15
  230.0 2.9 copy-start.20
  233.5 1.6 copy-start.18
  240.3 1.5 copy-start.26
  240.3 2.9 copy-start.38
  249.5 2.6 copy-start.34
  254.1 82.2 %copy-start.35 = (f32[192]{0:T(256)S(1)}, f32[192]{0:T(256)}, u32[]{:S(2)}) copy-start(f32[192]{0:T(256)} %param.27) | copy-start | bytes 2308
  254.2 82.2 %copy-start.36 = (f32[192]{0:T(256)S(1)}, f32[192]{0:T(256)}, u32[]{:S(2)}) copy-start(f32[192]{0:T(256)} %param.26) | copy-start | bytes 2308
  254.2 83.5 %copy-start.27 = (f32[8,128,128]{2,1,0:T(8,128)S(1)}, f32[8,128,128]{2,1,0:T(8,128)}, u32[]{:S(2)}) copy-start(f32[8,128,128]{2,1,0:T(8,128)} %param.22) | copy-start | bytes 1572868
  336.3 3.5 %copy-start.28 = (f32[8,128,128]{2,1,0:T(8,128)S(1)}, f32[8,128,128]{2,1,0:T(8,128)}, u32[]{:S(2)}) copy-start(f32[8,128,128]{2,1,0:T(8,128)} %param.21) | copy-start | bytes 1572868
  336.3 3.5 %copy-start.29 = (f32[8,128,128]{2,1,0:T(8,128)S(1)}, f32[8,128,128]{2,1,0:T(8,128)}, u32[]{:S(2)}) copy-start(f32[8,128,128]{2,1,0:T(8,128)} %param.20) | copy-start | bytes 1572868
  340.5 3.9 %copy-start.31 = (f32[8,128,128]{2,1,0:T(8,128)}, f32[8,128,128]{2,1,0:T(8,128)S(1)}, u32[]{:S(2)}) copy-start(f32[8,128,128]{2,1,0:T(8,128)S(1)} %get-tuple-element.104) | copy-start | bytes 1572868
  340.5 3.9 %copy-start.32 = (f32[8,128,128]{2,1,0:T(8,128)}, f32[8,128,128]{2,1,0:T(8,128)S(1)}, u32[]{:S(2)}) copy-start(f32[8,128,128]{2,1,0:T(8,128)S(1)} %get-tuple-element.103) | copy-start | bytes 1572868
  340.5 1.4 copy-start.24
  340.6 1.6 copy-start.30
  342.1 2.4 copy-start.22
  (7 other events, 7.8 us)
